TPU v7x, 256 devices: a whole 4x4x8 slice. The times are simulated.
256 devices in a mesh: tx: 16 (over x, y), ty: 16 (over z, core).
Axes of the slice: x: 4, y: 4, z: 8, core: 2. Of those that a mesh axis runs over, the one named last changes fastest.
Arguments:
- members: bfloat16 [128, 64, 512, 128], P('tx', 'ty'), may hold values from -4 to 4
- mean_state: float32 [128, 64, 512], P('tx', 'ty'), may hold values from -6 to 6
- obs_pert: bfloat16 [128, 64, 128, 128], P('tx', 'ty'), may hold values from -1.5 to 1.5
- obs_rinv: bfloat16 [128, 64, 128], P('tx', 'ty'), may hold values from 0.25 to 2
- innovation: bfloat16 [128, 64, 128], P('tx', 'ty'), may hold values from -12 to 12
- obs_count: int32 [128, 64], P('tx', 'ty'), may hold values from 1 to 128, as said below
- neighbours: int32 [128, 64, 12], P('tx', 'ty'), may hold values from 0 to 24, as said below
- loc_weight: float32 [128, 64, 12], P('tx', 'ty'), may hold values from 0.1 to 1
Outputs:
- analysis: bfloat16 [128, 64, 512, 128], P('tx', 'ty')
Inputs may be any that keep to these rules, and one draw needn't show every extreme that they name: `obs_count`: counts run from 1 to 128; 128 is reached on some blocks of every device. `neighbours`: the 12 codes of a group are distinct, each naming an offset (c // 5 - 2, c % 5 - 2) of at most two blocks per direction.
All inputs are finite; a program needn't handle non-finite values.
Results may differ from a plain program's by a relative error of at most 0.0049.
Values may be sent and summed in bfloat16 or wider, within the bound.
No kernel may reach another device: no remote copies, remote signals or barrier semaphores. Data moves between devices by JAX's collectives and lax.ppermute only.
A program may use at most 128 MiB of HBM per device.

v0:
```python
import jax
import jax.numpy as jnp
from jax import lax
from jax.experimental import pallas as pl
from jax.experimental.pallas import tpu as pltpu
from jax.sharding import Mesh
from jax.sharding import PartitionSpec as P

F32 = jnp.float32
BF16 = jnp.bfloat16
NSI = 5
WIDE = 3
ROWS = 144
BATCH_ROWS = 2
AXES = ("x", "y", "z", "c")
TX = ("x", "y")
TY = ("z", "c")


def ring(count, shift):
    return [(i, (i + shift) % count) for i in range(count)]


def split(value):
    high = value.astype(BF16)
    return high, (value - high.astype(F32)).astype(BF16)


def product(left, right):
    lhs = jnp.concatenate(left, axis=1)
    top = jnp.concatenate(right, axis=1)
    rhs = jnp.concatenate([top, top], axis=0)
    both = jnp.dot(lhs, rhs, preferred_element_type=F32)
    half = both.shape[1] // 2
    return both[:, :half] + both[:, half:]


def block_terms(block, gram_ref, vec_ref, slot):
    pert = block[:128]
    extra = block[128:].astype(F32)
    weight, innov = extra[0:1], extra[1:2]
    scaled = (pert.astype(F32).T * weight).astype(BF16)
    high, low = split(weight * innov)
    line = lax.broadcasted_iota(jnp.int32, (16, 128), 0)
    tail = jnp.where(
        line == 0,
        jnp.broadcast_to(high.astype(F32), (16, 128)),
        jnp.where(line == 1, jnp.broadcast_to(low.astype(F32), (16, 128)), 0.0),
    ).astype(BF16)
    lhs = jnp.concatenate([scaled, tail], axis=0)
    terms = jnp.dot(lhs, pert, preferred_element_type=F32)
    gram_ref[slot] = terms[:128]
    vec_ref[slot] = terms[128:136]


def make_kernel(gx, gy, cl, listed):
    outer_y = gy + 2 * WIDE
    ring_y = gy + 2
    batch = BATCH_ROWS * ring_y
    batches = (gx + 2) // BATCH_ROWS

    def kernel(
        target_ref, factor_ref, shift_ref,
        own_ref, low_ref, high_ref, left_ref, right_ref, cleft_ref, cright_ref,
        mean_ref, members_ref, out_ref,
        gram_ref, vec_ref, weight_ref, root_ref, inv_ref, upd_ref, side_ref, norm_ref,
        held_ref, stage_ref, in_sem, out_sem,
    ):
        fetch = pltpu.make_async_copy(members_ref, held_ref, in_sem)
        fetch.start()

        def piece(ref, row0, col0, rows_split=None):
            nrow, ncol = ref.shape[0], ref.shape[1]

            @pl.loop(0, nrow)
            def _(r):
                if rows_split is None:
                    base = (r + row0) * outer_y
                else:
                    base = (r + jnp.where(r >= rows_split, gx, 0) + row0) * outer_y
                for c in range(ncol):
                    block_terms(ref[r, c], gram_ref, vec_ref, base + (col0 + c))

        piece(own_ref, WIDE, WIDE)
        piece(low_ref, 0, WIDE)
        piece(high_ref, WIDE + gx, WIDE)
        piece(left_ref, WIDE, 0)
        piece(right_ref, WIDE, WIDE + gy)
        piece(cleft_ref, 0, 0, WIDE)
        piece(cright_ref, 0, WIDE + gy, WIDE)

        eye = (
            lax.broadcasted_iota(jnp.int32, (128, 128), 0)
            == lax.broadcasted_iota(jnp.int32, (128, 128), 1)
        )
        shift = shift_ref[0]

        def update_of(value, g):
            upd = jnp.where(eye, 1.5, 0.0) - 0.5 * value
            high, low = split(upd)
            upd_ref[g, 0] = high
            upd_ref[g, 1] = low

        def keep(ref, g, value):
            high, low = split(value)
            ref[g, 0] = high
            ref[g, 1] = low

        def pair(ref, g):
            return ref[g, 0], ref[g, 1]

        @pl.loop(0, batches)
        def _(b):
            for g in range(batch):
                line = b * batch + g
                total = jnp.zeros((128, 128), F32)
                vsum = jnp.zeros((8, 128), F32)
                for j in range(listed):
                    slot = target_ref[line, j]
                    factor = factor_ref[line, j]
                    total = total + factor * gram_ref[slot]
                    vsum = vsum + factor * vec_ref[slot]
                matrix = total + jnp.where(eye, shift, 0.0)
                norm = jnp.sqrt(jnp.sum(matrix * matrix, keepdims=True))
                norm_ref[g] = jnp.broadcast_to(norm, (8, 128))
                root = matrix / norm
                keep(root_ref, g, root)
                update_of(root, g)
                vrow = vsum[0:1] + vsum[1:2]
                side = jnp.broadcast_to(vrow, (128, 128)).T
                keep(side_ref, g, side)
            for g in range(batch):
                upd = pair(upd_ref, g)
                inv_ref[g, 0] = upd[0]
                inv_ref[g, 1] = upd[1]
                keep(root_ref, g, product(pair(root_ref, g), upd))
            for step in range(1, NSI):
                for g in range(batch):
                    update_of(product(pair(inv_ref, g), pair(root_ref, g)), g)
                for g in range(batch):
                    upd = pair(upd_ref, g)
                    if step < NSI - 1:
                        inv, root = pair(inv_ref, g), pair(root_ref, g)
                        stacked = tuple(
                            jnp.concatenate([i, r], axis=0) for i, r in zip(inv, root)
                        )
                        both = product(stacked, upd)
                        keep(inv_ref, g, both[:128])
                        keep(root_ref, g, both[128:])
                    else:
                        inv = product(pair(inv_ref, g), upd)
                        keep(inv_ref, g, inv)
                        weight_ref[b * batch + g] = inv
            for g in range(batch):
                keep(side_ref, g, product(pair(inv_ref, g), pair(side_ref, g)))
            for g in range(batch):
                line = b * batch + g
                norm = norm_ref[g][0:1]
                wbar = product(pair(inv_ref, g), pair(side_ref, g)) / norm
                scale = jnp.sqrt(F32(127.0)) / jnp.sqrt(norm)
                weight_ref[line] = scale * weight_ref[line] + wbar

        fetch.wait()
        empty = jnp.zeros((128, 128), BF16)

        @pl.loop(0, gx)
        def _(r):
            for p in range(gy // 2):
                blends = []
                for c in (2 * p, 2 * p + 1):
                    at = (r + 1) * ring_y + (c + 1)
                    blend = (
                        4.0 * weight_ref[at]
                        + weight_ref[at + ring_y]
                        + weight_ref[at - ring_y]
                        + weight_ref[at + 1]
                        + weight_ref[at - 1]
                    ) * 0.125
                    blends.append(blend.astype(BF16))
                rhs = jnp.concatenate(
                    [
                        jnp.concatenate([blends[0], empty], axis=1),
                        jnp.concatenate([empty, blends[1]], axis=1),
                    ],
                    axis=0,
                )
                mean = mean_ref[r].T
                lhs = jnp.concatenate([held_ref[r, 2 * p], held_ref[r, 2 * p + 1]], axis=1)
                both = jnp.dot(lhs, rhs, preferred_element_type=F32)
                for side in range(2):
                    c = 2 * p + side
                    value = both[:, 128 * side : 128 * side + 128] + mean[:, c : c + 1]
                    stage_ref[r, c] = value.astype(BF16)
            pltpu.make_async_copy(stage_ref.at[r], out_ref.at[r], out_sem.at[r]).start()

        @pl.loop(0, gx)
        def _(r):
            pltpu.make_async_copy(stage_ref.at[r], out_ref.at[r], out_sem.at[r]).wait()

    return kernel


def analyse(target, factor, shift, pieces, mean, members):
    gx, gy, cl, width = members.shape
    listed = target.shape[1]
    outer = (gx + 2 * WIDE) * (gy + 2 * WIDE)
    ring_count = (gx + 2) * (gy + 2)
    batch = BATCH_ROWS * (gy + 2)
    vmem = pl.BlockSpec(memory_space=pltpu.VMEM)
    smem = pl.BlockSpec(memory_space=pltpu.SMEM)
    hbm = pl.BlockSpec(memory_space=pl.ANY)
    halves = pltpu.VMEM((batch, 2, width, width), BF16)
    return pl.pallas_call(
        make_kernel(gx, gy, cl, listed),
        name="analyse",
        out_shape=jax.ShapeDtypeStruct(members.shape, BF16),
        in_specs=[smem] * 3 + [vmem] * 8 + [hbm],
        out_specs=hbm,
        scratch_shapes=[
            pltpu.VMEM((outer, width, width), F32),
            pltpu.VMEM((outer, 8, width), F32),
            pltpu.VMEM((ring_count, width, width), F32),
            halves, halves, halves, halves,
            pltpu.VMEM((batch, 8, width), F32),
            pltpu.VMEM(members.shape, BF16),
            pltpu.VMEM(members.shape, BF16),
            pltpu.SemaphoreType.DMA,
            pltpu.SemaphoreType.DMA((gx,)),
        ],
        compiler_params=pltpu.CompilerParams(vmem_limit_bytes=44 * 2**20),
    )(target, factor, shift, *pieces, mean, members)


def pack(obs_pert, obs_weight, innovation, neighbours, loc_weight):
    gx, gy, slot_count, width = obs_pert.shape
    listed = neighbours.shape[-1]
    first = lax.reduce_precision(loc_weight, 8, 7)
    rest = loc_weight - first
    second = lax.reduce_precision(rest, 8, 7)
    third = rest - second
    small = jnp.stack([neighbours.astype(F32), first, second, third], axis=2)
    small = jnp.pad(small, ((0, 0), (0, 0), (0, 0), (0, width - listed)))
    extra = jnp.concatenate(
        [
            obs_weight[:, :, None, :].astype(BF16),
            innovation[:, :, None, :],
            small.astype(BF16),
            jnp.zeros((gx, gy, ROWS - slot_count - 6, width), BF16),
        ],
        axis=2,
    )
    return jnp.concatenate([obs_pert, extra], axis=2)


def lists(pieces, gx, gy, listed):
    own, low, high, left, right, cleft, cright = (p[:, :, 130:134, :listed] for p in pieces)
    low, high = low[-1:], high[:1]
    left, right = left[:, -1:], right[:, :1]
    cleft = cleft[WIDE - 1 : WIDE + 1, -1:]
    cright = cright[WIDE - 1 : WIDE + 1, :1]
    middle = jnp.concatenate([left, own, right], axis=1)
    top = jnp.concatenate([cleft[:1], low, cright[:1]], axis=1)
    bottom = jnp.concatenate([cleft[1:], high, cright[1:]], axis=1)
    framed = jnp.concatenate([top, middle, bottom], axis=0).astype(F32)
    codes = framed[:, :, 0].astype(jnp.int32)
    factor = framed[:, :, 1] + framed[:, :, 2] + framed[:, :, 3]
    outer_y = gy + 2 * WIDE
    row = jnp.arange(gx + 2, dtype=jnp.int32)[:, None, None]
    col = jnp.arange(gy + 2, dtype=jnp.int32)[None, :, None]
    target = (row + codes // 5) * outer_y + col + codes % 5
    return target.reshape(-1, listed), factor.reshape(-1, listed)


def total_of(values):
    count = lax.axis_size("c")
    values = values + lax.ppermute(values, "c", ring(count, 1))
    chips = lax.axis_size("x") * lax.axis_size("y") * lax.axis_size("z")
    sent = jnp.broadcast_to(values, (chips, values.shape[1]))
    return jnp.sum(lax.all_to_all(sent, ("x", "y", "z"), 0, 0, tiled=True), axis=0)


def shards(members, mean_state, obs_pert, obs_rinv, innovation, obs_count, neighbours, loc_weight):
    gx, gy, slot_count, width = obs_pert.shape
    listed = neighbours.shape[-1]
    slots = jnp.arange(slot_count, dtype=jnp.int32)
    live_slot = slots[None, None, :] < obs_count[:, :, None]
    obs_weight = jnp.where(live_slot, obs_rinv.astype(F32), F32(0.0))
    own = pack(obs_pert, obs_weight, innovation, neighbours, loc_weight)
    tx, ty = lax.axis_size(TX), lax.axis_size(TY)
    low = lax.ppermute(own[gx - WIDE :], TX, ring(tx, 1))
    high = lax.ppermute(own[:WIDE], TX, ring(tx, -1))
    left = lax.ppermute(own[:, gy - WIDE :], TY, ring(ty, 1))
    right = lax.ppermute(own[:, :WIDE], TY, ring(ty, -1))
    cleft = lax.ppermute(
        jnp.concatenate([low[:, gy - WIDE :], high[:, gy - WIDE :]], axis=0), TY, ring(ty, 1)
    )
    cright = lax.ppermute(
        jnp.concatenate([low[:, :WIDE], high[:, :WIDE]], axis=0), TY, ring(ty, -1)
    )
    innov_f = innovation.astype(F32)
    square_sum = jnp.sum(jnp.square(obs_pert.astype(F32)), axis=-1)
    first = jnp.sum(obs_weight * innov_f * innov_f)
    second = jnp.sum(live_slot.astype(F32) + obs_weight * square_sum / (width - 1))
    lane = lax.broadcasted_iota(jnp.int32, (1, 128), 1)
    sums = total_of(jnp.where(lane == 0, first, jnp.where(lane == 1, second, 0.0)))
    shift = (width - 1) / (sums[0] / sums[1])
    pieces = (own, low, high, left, right, cleft, cright)
    target, factor = lists(pieces, gx, gy, listed)
    return analyse(target, factor, shift.reshape(1), pieces, mean_state, members)


def solution(mesh):
    finer = Mesh(mesh.devices.reshape(4, 4, 8, 2), AXES)
    return jax.shard_map(
        shards,
        mesh=finer,
        in_specs=(
            P(TX, TY, None, None),
            P(TX, TY, None),
            P(TX, TY, None, None),
            P(TX, TY, None),
            P(TX, TY, None),
            P(TX, TY),
            P(TX, TY, None),
            P(TX, TY, None),
        ),
        out_specs=P(TX, TY, None, None),
        check_vma=False,
    )
```

profile of v0, /device:TPU:1, one launch (start us, length us, event | category | flops | bytes accessed | tf_op | source)
XLA Modules:
  0.0 103.8 jit_solution(15189708225835944748)
XLA Ops:
  0.0 0.0 copy-start.2
  0.0 0.8 copy.69
  0.8 0.7 fusion.17
  1.6 0.7 copy.80
  2.3 1.8 %multiply_reduce_fusion = f32[8,4,128]{2,1,0:T(4,128)S(1)} fusion(bf16[8,4,128,128]{3,2,1,0:T(8,128)(2,1)} %param.10), kind=kLoop, calls=%fused_computation | loop fusion | flops 1568768 | bytes 1064960 | tf_op jit(solution)/shard_map/reduce_sum | solution.py:301
  4.2 1.5 %fusion.13 = (f32[]{:T(128)}, f32[]{:T(128)}, bf16[8,4,1,128]{3,1,0,2:T(4,128)(2,1)S(1)}) fusion(bf16[8,4,128]{2,1,0:T(4,128)(2,1)} %param.12, bf16[8,4,128]{2,1,0:T(4,128)(2,1)} %param.11, s32[8,4]{1,0:T(8,128)S(1)} %copy.69, f32[8,4,128]{2,1,0:T(4,128)S(1)} %multiply_reduce_fusion), kind=kLoop, calls=%fused_computation.31 | loop fusion | flops 53246 | bytes 41096 | tf_op jit(solution)/shard_map/reduce_sum | solution.py:302
  5.7 0.7 fusion.19
  6.4 0.1 fusion.10
  6.6 0.0 copy-done.2
  6.6 0.8 concatenate.21.own_ref
  7.4 0.1 fusion.22
  7.5 5.8 %collective-permute-start.1 = (bf16[3,4,144,128]{3,2,1,0:T(8,128)(2,1)S(1)}, bf16[3,4,144,128]{3,2,1,0:T(8,128)(2,1)S(1)}, u32[]{:S(2)}, u32[]{:S(2)}) collective-permute-start(bf16[3,4,144,128]{3,2,1,0:T(8,128)(2,1)S(1)} %get-tuple-element.12), channel_id=1, source_target_pairs={{0,240},{16,0},{32,16},{48,32},{64,48},{80,64},{96,80},{112,96},{1... | collective-permute-start | bytes 1327112 | tf_op jit(solution)/shard_map/ppermute | solution.py:291
  13.3 0.0 collective-permute-start
  13.3 1.4 %fusion.21 = (bf16[8,3,144,128]{3,2,1,0:T(8,128)(2,1)}, bf16[8,3,144,128]{3,2,1,0:T(8,128)(2,1)}) fusion(bf16[8,4,144,128]{3,2,1,0:T(8,128)(2,1)S(1)} %concatenate.21.own_ref), kind=kLoop, calls=%fused_computation.46 | loop fusion | bytes 3538944 | tf_op jit(solution)/shard_map/slice | solution.py:292
  14.8 2.5 %collective-permute-start.4 = (bf16[8,3,144,128]{3,2,1,0:T(8,128)(2,1)}, bf16[8,3,144,128]{3,2,1,0:T(8,128)(2,1)S(1)}, u32[]{:S(2)}, u32[]{:S(2)}) collective-permute-start(bf16[8,3,144,128]{3,2,1,0:T(8,128)(2,1)} %get-tuple-element.9), channel_id=1, source_target_pairs={{0,1},{1,2},{2,3},{3,4},{4,5},{5,6},{6,7},{7,8},{8,9},{9,10},{10,1... | collective-permute-start | bytes 2654216 | tf_op jit(solution)/shard_map/ppermute | solution.py:292
  17.2 0.0 collective-permute-start.5
  17.2 4.9 %collective-permute-done.1.high_ref = bf16[3,4,144,128]{3,2,1,0:T(8,128)(2,1)S(1)} collective-permute-done((bf16[3,4,144,128]{3,2,1,0:T(8,128)(2,1)S(1)}, bf16[3,4,144,128]{3,2,1,0:T(8,128)(2,1)S(1)}, u32[]{:S(2)}, u32[]{:S(2)}) %collective-permute-start.1) | collective-permute-done | bytes 442400 | tf_op jit(solution)/shard_map/ppermute | solution.py:291
  22.2 0.1 fusion.26
  22.3 5.2 %collective-permute-done.low_ref = bf16[3,4,144,128]{3,2,1,0:T(8,128)(2,1)S(1)} collective-permute-done((bf16[3,4,144,128]{3,2,1,0:T(8,128)(2,1)S(1)}, bf16[3,4,144,128]{3,2,1,0:T(8,128)(2,1)S(1)}, u32[]{:S(2)}, u32[]{:S(2)}) %collective-permute-start) | collective-permute-done | bytes 442400 | tf_op jit(solution)/shard_map/ppermute | solution.py:290
  27.4 0.1 fusion.25
  27.5 0.0 copy-start.1
  27.5 0.9 pad_maximum_fusion.1
  28.4 1.8 %collective-permute-start.3 = (bf16[6,3,144,128]{3,2,1,0:T(8,128)(2,1)}, bf16[6,3,144,128]{3,2,1,0:T(8,128)(2,1)}, u32[]{:S(2)}, u32[]{:S(2)}) collective-permute-start(bf16[6,3,144,128]{3,2,1,0:T(8,128)(2,1)} %pad_maximum_fusion.1), channel_id=1, source_target_pairs={{0,15},{1,0},{2,1},{3,2},{4,3},{5,4},{6,5},{7,6},{8,7},{9,8},{10,9... | collective-permute-start | bytes 1990664 | tf_op jit(solution)/shard_map/ppermute | solution.py:297
  30.2 1.3 %compare_select_fusion.1 = f32[1,128]{1,0:T(1,128)S(1)} fusion(f32[]{:T(128)} %get-tuple-element.8, f32[]{:T(128)} %get-tuple-element.7), kind=kLoop, calls=%fused_computation.44 | loop fusion | flops 512 | bytes 520 | tf_op jit(solution)/shard_map/jit(_where)/select_n | solution.py:305
  31.5 4.2 %collective-permute-start.6 = (f32[1,128]{1,0:T(1,128)S(1)}, f32[1,128]{1,0:T(1,128)S(1)}, u32[]{:S(2)}, u32[]{:S(2)}) collective-permute-start(f32[1,128]{1,0:T(1,128)S(1)} %compare_select_fusion.1), channel_id=1, source_target_pairs={{0,1},{1,0},{2,3},{3,2},{4,5},{5,4},{6,7},{7,6},{8,9},{9,8},{10,11... | collective-permute-start | bytes 1544 | tf_op jit(solution)/shard_map/ppermute | solution.py:276
  35.7 0.9 pad_maximum_fusion
  36.7 0.0 collective-permute-start.2
  36.7 0.0 collective-permute-done.6
  36.7 1.3 %add_bitcast_fusion = f32[128]{0:T(128)S(1)} fusion(f32[1,128]{1,0:T(1,128)S(1)} %collective-permute-done.6, f32[]{:T(128)} %get-tuple-element.8, f32[]{:T(128)} %get-tuple-element.7), kind=kLoop, calls=%fused_computation.45 | loop fusion | flops 640 | bytes 1032 | tf_op jit(solution)/shard_map/add | solution.py:276
  37.9 0.6 broadcast_in_dim.38
  38.6 7.6 %all-to-all-start = ((f32[128,1,128]{2,1,0:T(1,128)}), f32[128,1,128]{2,1,0:T(1,128)S(1)}, u32[]{:S(2)}, u32[]{:S(2)}) async-start(f32[128,1,128]{2,1,0:T(1,128)} %broadcast_in_dim.38), calls=%async_computation | async-start | bytes 131072 | tf_op jit(solution)/shard_map/all_to_all | solution.py:279
  46.2 0.1 add.66
  46.2 0.1 add.62
  46.3 10.5 %all-to-all-done = f32[128,1,128]{2,1,0:T(1,128)S(1)} async-done(((f32[128,1,128]{2,1,0:T(1,128)}), f32[128,1,128]{2,1,0:T(1,128)S(1)}, u32[]{:S(2)}, u32[]{:S(2)}) %all-to-all-start) | async-done | bytes 65568 | tf_op jit(solution)/shard_map/all_to_all | solution.py:279
  56.9 0.7 fusion.27
  58.9 0.0 collective-permute-done.4.left_ref
  58.9 0.0 collective-permute-done.5.right_ref
  58.9 0.7 slice.119
  59.7 0.0 collective-permute-done.3.cright_ref
  59.7 0.7 fusion.24
  60.4 0.0 collective-permute-done.2.cleft_ref
  60.4 0.7 fusion.23
  61.1 0.1 maximum_convert_fusion
  61.2 0.2 compare_reduce_fusion
  61.3 0.1 fusion.11
  61.5 0.3 remainder_reduce_fusion
  61.8 0.1 fusion.7.target_ref
  61.9 0.0 copy-done.1
  61.9 0.0 copy-start
  61.9 2.2 %copy-done = bf16[8,4,512,128]{3,2,1,0:T(8,128)(2,1)S(1)} copy-done((bf16[8,4,512,128]{3,2,1,0:T(8,128)(2,1)S(1)}, bf16[8,4,512,128]{3,2,1,0:T(8,128)(2,1)}, u32[]{:S(2)}) %copy-start) | copy-done | bytes 4194328
  64.1 39.5 %analyse.1 = bf16[8,4,512,128]{3,2,1,0:T(8,128)(2,1)} custom-call(s32[60,12]{1,0:T(8,128)S(1)} %fusion.7.target_ref, f32[60,12]{1,0:T(8,128)S(1)} %add.73.factor_ref, f32[1]{0:T(128)S(6)} %div.25.shift_ref, bf16[8,4,144,128]{3,2,1,0:T(8,128)(2,1)S(1)} %concatenate.21.own_ref, bf16[3,4,144,128]{3,2,1,0:T(8,128)(2,1)S(1)} %collective-permute-done.low_ref, ...), custom_call_target="tpu_custom_call" | custom-call | tf_op jit(solution)/shard_map/analyse/pallas_call | solution.py:213
  (16 shorter events, 0.2 us)
Async XLA Ops:
  0.0 6.6 %copy-start.2 = (bf16[8,4,128,128]{3,2,1,0:T(8,128)(2,1)S(1)}, bf16[8,4,128,128]{3,2,1,0:T(8,128)(2,1)}, u32[]{:S(2)}) copy-start(bf16[8,4,128,128]{3,2,1,0:T(8,128)(2,1)} %param.10) | copy-start | bytes 3145732
  7.5 14.7 %collective-permute-start.1 = (bf16[3,4,144,128]{3,2,1,0:T(8,128)(2,1)S(1)}, bf16[3,4,144,128]{3,2,1,0:T(8,128)(2,1)S(1)}, u32[]{:S(2)}, u32[]{:S(2)}) collective-permute-start(bf16[3,4,144,128]{3,2,1,0:T(8,128)(2,1)S(1)} %get-tuple-element.12), channel_id=1, source_target_pairs={{0,240},{16,0},{32,16},{48,32},{64,48},{80,64},{96,80},{112,96},{1... | collective-permute-start | bytes 1327112 | tf_op jit(solution)/shard_map/ppermute | solution.py:291
  13.3 14.1 %collective-permute-start = (bf16[3,4,144,128]{3,2,1,0:T(8,128)(2,1)S(1)}, bf16[3,4,144,128]{3,2,1,0:T(8,128)(2,1)S(1)}, u32[]{:S(2)}, u32[]{:S(2)}) collective-permute-start(bf16[3,4,144,128]{3,2,1,0:T(8,128)(2,1)S(1)} %get-tuple-element.11), channel_id=1, source_target_pairs={{0,16},{16,32},{32,48},{48,64},{64,80},{80,96},{96,112},{112,128},... | collective-permute-start | bytes 1327112 | tf_op jit(solution)/shard_map/ppermute | solution.py:290
  14.8 44.1 %collective-permute-start.4 = (bf16[8,3,144,128]{3,2,1,0:T(8,128)(2,1)}, bf16[8,3,144,128]{3,2,1,0:T(8,128)(2,1)S(1)}, u32[]{:S(2)}, u32[]{:S(2)}) collective-permute-start(bf16[8,3,144,128]{3,2,1,0:T(8,128)(2,1)} %get-tuple-element.9), channel_id=1, source_target_pairs={{0,1},{1,2},{2,3},{3,4},{4,5},{5,6},{6,7},{7,8},{8,9},{9,10},{10,1... | collective-permute-start | bytes 2654216 | tf_op jit(solution)/shard_map/ppermute | solution.py:292
  17.2 41.7 %collective-permute-start.5 = (bf16[8,3,144,128]{3,2,1,0:T(8,128)(2,1)}, bf16[8,3,144,128]{3,2,1,0:T(8,128)(2,1)}, u32[]{:S(2)}, u32[]{:S(2)}) collective-permute-start(bf16[8,3,144,128]{3,2,1,0:T(8,128)(2,1)} %get-tuple-element.10), channel_id=1, source_target_pairs={{0,15},{1,0},{2,1},{3,2},{4,3},{5,4},{6,5},{7,6},{8,7},{9,8},{10,9... | collective-permute-start | bytes 2654216 | tf_op jit(solution)/shard_map/ppermute | solution.py:293
  27.5 34.4 %copy-start.1 = (f32[8,4,512]{2,1,0:T(4,128)S(1)}, f32[8,4,512]{2,1,0:T(4,128)}, u32[]{:S(2)}) copy-start(f32[8,4,512]{2,1,0:T(4,128)} %mean_ref.1) | copy-start | bytes 196612
  28.4 31.3 %collective-permute-start.3 = (bf16[6,3,144,128]{3,2,1,0:T(8,128)(2,1)}, bf16[6,3,144,128]{3,2,1,0:T(8,128)(2,1)}, u32[]{:S(2)}, u32[]{:S(2)}) collective-permute-start(bf16[6,3,144,128]{3,2,1,0:T(8,128)(2,1)} %pad_maximum_fusion.1), channel_id=1, source_target_pairs={{0,15},{1,0},{2,1},{3,2},{4,3},{5,4},{6,5},{7,6},{8,7},{9,8},{10,9... | collective-permute-start | bytes 1990664 | tf_op jit(solution)/shard_map/ppermute | solution.py:297
  31.5 5.2 %collective-permute-start.6 = (f32[1,128]{1,0:T(1,128)S(1)}, f32[1,128]{1,0:T(1,128)S(1)}, u32[]{:S(2)}, u32[]{:S(2)}) collective-permute-start(f32[1,128]{1,0:T(1,128)S(1)} %compare_select_fusion.1), channel_id=1, source_target_pairs={{0,1},{1,0},{2,3},{3,2},{4,5},{5,4},{6,7},{7,6},{8,9},{9,8},{10,11... | collective-permute-start | bytes 1544 | tf_op jit(solution)/shard_map/ppermute | solution.py:276
  36.7 23.7 %collective-permute-start.2 = (bf16[6,3,144,128]{3,2,1,0:T(8,128)(2,1)}, bf16[6,3,144,128]{3,2,1,0:T(8,128)(2,1)}, u32[]{:S(2)}, u32[]{:S(2)}) collective-permute-start(bf16[6,3,144,128]{3,2,1,0:T(8,128)(2,1)} %pad_maximum_fusion), channel_id=1, source_target_pairs={{0,1},{1,2},{2,3},{3,4},{4,5},{5,6},{6,7},{7,8},{8,9},{9,10},{10,1... | collective-permute-start | bytes 1990664 | tf_op jit(solution)/shard_map/ppermute | solution.py:294
  38.6 18.3 %all-to-all-start = ((f32[128,1,128]{2,1,0:T(1,128)}), f32[128,1,128]{2,1,0:T(1,128)S(1)}, u32[]{:S(2)}, u32[]{:S(2)}) async-start(f32[128,1,128]{2,1,0:T(1,128)} %broadcast_in_dim.38), calls=%async_computation | async-start | bytes 131072 | tf_op jit(solution)/shard_map/all_to_all | solution.py:279
  61.9 2.2 %copy-start = (bf16[8,4,512,128]{3,2,1,0:T(8,128)(2,1)S(1)}, bf16[8,4,512,128]{3,2,1,0:T(8,128)(2,1)}, u32[]{:S(2)}) copy-start(bf16[8,4,512,128]{3,2,1,0:T(8,128)(2,1)} %members_ref.1) | copy-start | bytes 12582916
where the time goes:
time: 104 us
  Pallas kernels  39.5 us (38%)
  starting transfers between devices  21.9 us (21%)
  waiting for transfers between devices  20.7 us (20%)
  other arithmetic  10 us (10%)
  local copies, waits for them, and re-layouts  9.95 us (10%)
  between operations  1.7 us (2%)
    pallas_call x1, Pallas kernels, analyse(): pl.pallas_call(make_kernel(gx, gy, cl, listed), name='analyse', out_shape...  39.5 us
    all_to_all x1, waiting for transfers between devices, total_of(): lax.all_to_all(sent, ('x', 'y', 'z'), 0, 0, tiled=True)  10.5 us
    all_to_all x1, starting transfers between devices, total_of(): lax.all_to_all(sent, ('x', 'y', 'z'), 0, 0, tiled=True)  7.57 us
    ppermute x1, starting transfers between devices, shards(): high = lax.ppermute(own[:WIDE], TX, ring(tx, -1))  5.82 us
    ppermute x1, waiting for transfers between devices, shards(): low = lax.ppermute(own[gx - WIDE:], TX, ring(tx, 1))  5.16 us
    ppermute x1, waiting for transfers between devices, shards(): high = lax.ppermute(own[:WIDE], TX, ring(tx, -1))  4.94 us
    ppermute x1, starting transfers between devices, total_of(): values = values + lax.ppermute(values, 'c', ring(count, 1))  4.25 us
    unnamed x7, local copies, waits for them, and re-layouts  3.04 us
  transfers between devices with their start and end apart: 8, of which 3 were waited for; matrix products, arithmetic and copies ran while one was open for 9% of the time, Pallas kernels for 0%

commit v1 on v0

v1 whole, which is shorter than its diff:
```python
import jax
import jax.numpy as jnp
from jax import lax
from jax.experimental import pallas as pl
from jax.experimental.pallas import tpu as pltpu
from jax.sharding import Mesh
from jax.sharding import PartitionSpec as P

F32 = jnp.float32
BF16 = jnp.bfloat16
NSI = 5
WIDE = 3
ROWS = 144
BATCH = 14
PREPARE_VMEM = 56 * 2**20
ANALYSE_VMEM = 59 * 2**20
AXES = ("x", "y", "z", "c")
TX = ("x", "y")
TY = ("z", "c")


def ring(count, shift):
    return [(i, (i + shift) % count) for i in range(count)]


def split(value):
    high = value.astype(BF16)
    return high, (value - high.astype(F32)).astype(BF16)


def product(left, right):
    lhs = jnp.concatenate(left, axis=1)
    top = jnp.concatenate(right, axis=1)
    rhs = jnp.concatenate([top, top], axis=0)
    both = jnp.dot(lhs, rhs, preferred_element_type=F32)
    half = both.shape[1] // 2
    return both[:, :half] + both[:, half:]


def block_terms(block, gram_ref, vec_ref, slot):
    pert = block[:128]
    extra = block[128:].astype(F32)
    weight, innov = extra[0:1], extra[1:2]
    scaled = (pert.astype(F32).T * weight).astype(BF16)
    high, low = split(weight * innov)
    line = lax.broadcasted_iota(jnp.int32, (16, 128), 0)
    tail = jnp.where(
        line == 0,
        jnp.broadcast_to(high.astype(F32), (16, 128)),
        jnp.where(line == 1, jnp.broadcast_to(low.astype(F32), (16, 128)), 0.0),
    ).astype(BF16)
    lhs = jnp.concatenate([scaled, tail], axis=0)
    terms = jnp.dot(lhs, pert, preferred_element_type=F32)
    gram_ref[slot] = terms[:128]
    vec_ref[slot] = terms[128:136]


def prepare_kernel(
    pert_hbm, rinv_hbm, innov_hbm, count_ref, codes_hbm, factor_hbm,
    own_ref, low_ref, high_ref, left_ref, right_ref, sums_ref,
    extra_ref, pert_ref, rinv_ref, innov_ref, codes_ref, factor_ref, sems,
):
    copies = [
        pltpu.make_async_copy(src, dst, sems.at[k])
        for k, (src, dst) in enumerate(
            [
                (rinv_hbm, rinv_ref), (innov_hbm, innov_ref), (codes_hbm, codes_ref),
                (factor_hbm, factor_ref), (pert_hbm, pert_ref),
            ]
        )
    ]
    for copy in copies:
        copy.start()
    gx, gy = own_ref.shape[:2]
    lane = lax.broadcasted_iota(jnp.int32, (1, 128), 1)
    listed = codes_ref.shape[-1]
    extra_ref[...] = jnp.zeros(extra_ref.shape, F32)
    first = jnp.zeros((1, 128), F32)
    alive = jnp.zeros((1, 128), F32)
    spread = jnp.zeros((8, 128), F32)
    for copy in copies:
        copy.wait()
    for r in range(gx):
        rinv = rinv_ref[r].astype(F32)
        innovs = innov_ref[r].astype(F32)
        codes = codes_ref[r].astype(F32)
        whole = factor_ref[r]
        one = whole.astype(BF16).astype(F32)
        two = (whole - one).astype(BF16).astype(F32)
        three = whole - one - two
        for c in range(gy):
            n = r * gy + c
            live = lane < count_ref[c, r]
            weight = jnp.where(live, rinv[c : c + 1], 0.0)
            innov = innovs[c : c + 1]
            extra_ref[n, 0:1, :] = weight
            extra_ref[n, 1:2, :] = innov
            extra_ref[n, 2:3, :listed] = codes[c : c + 1]
            extra_ref[n, 3:4, :listed] = one[c : c + 1]
            extra_ref[n, 4:5, :listed] = two[c : c + 1]
            extra_ref[n, 5:6, :listed] = three[c : c + 1]
            block = pert_ref[r, c]
            turned = block.astype(F32).T
            part = turned * turned * weight
            for k in range(16):
                spread = spread + part[8 * k : 8 * k + 8]
            first = first + weight * innov * innov
            alive = alive + jnp.where(live, 1.0, 0.0)
            places = [(own_ref, r, c)]
            if r >= gx - WIDE:
                places.append((low_ref, r - (gx - WIDE), c))
            if r < WIDE:
                places.append((high_ref, r, c))
            if c >= gy - WIDE:
                places.append((left_ref, r, c - (gy - WIDE)))
            if c < WIDE:
                places.append((right_ref, r, c))
            tile = extra_ref[n].astype(BF16)
            for ref, i, j in places:
                ref[i, j, :128] = block
                ref[i, j, 128:] = tile
    s1 = jnp.sum(first, keepdims=True)
    s2 = jnp.sum(alive, keepdims=True) + jnp.sum(spread, keepdims=True) / 127.0
    sums = jnp.where(lane == 0, s1, jnp.where(lane == 1, s2, 0.0))
    sums_ref[...] = jnp.broadcast_to(sums.reshape(1, 1, 128), sums_ref.shape)


def prepare(obs_pert, obs_rinv, innovation, obs_count, neighbours, loc_weight, devices):
    gx, gy, _, width = obs_pert.shape
    vmem = pl.BlockSpec(memory_space=pltpu.VMEM)
    hbm = pl.BlockSpec(memory_space=pltpu.HBM)
    smem = pl.BlockSpec(memory_space=pltpu.SMEM)

    def blocks(rows, cols):
        return jax.ShapeDtypeStruct((rows, cols, ROWS, width), BF16)

    return pl.pallas_call(
        prepare_kernel,
        name="prepare",
        out_shape=[
            blocks(gx, gy), blocks(WIDE, gy), blocks(WIDE, gy), blocks(gx, WIDE), blocks(gx, WIDE),
            jax.ShapeDtypeStruct((devices, 1, width), F32),
        ],
        in_specs=[hbm, hbm, hbm, smem, hbm, hbm],
        out_specs=[vmem] * 6,
        scratch_shapes=[pltpu.VMEM((gx * gy, 16, width), F32)]
        + [
            pltpu.VMEM(x.shape, x.dtype)
            for x in (obs_pert, obs_rinv, innovation, neighbours, loc_weight)
        ]
        + [pltpu.SemaphoreType.DMA((5,))],
        compiler_params=pltpu.CompilerParams(vmem_limit_bytes=PREPARE_VMEM),
    )(obs_pert, obs_rinv, innovation, obs_count.T, neighbours, loc_weight)


def gram_loop(parts, gram_ref, vec_ref):
    rows = parts[0][0].shape[0]

    @pl.loop(0, rows)
    def _(r):
        for ref, base_of in parts:
            base = base_of(r)
            for c in range(ref.shape[1]):
                block_terms(ref[r, c], gram_ref, vec_ref, base + c)


def sliced(ref, base_of, pieces):
    rows = ref.shape[0] // pieces
    return [
        (ref.at[pl.ds(k * rows, rows)], lambda r, at=k * rows: base_of(r + at))
        for k in range(pieces)
    ]


def group_lines(gx, gy):
    inner = [(r, c) for r in range(gx) for c in range(gy)]
    edge = [(-1, c) for c in range(gy)] + [(gx, c) for c in range(gy)]
    edge += [(r, -1) for r in range(gx)] + [(r, gy) for r in range(gx)]
    return [(r + 1, c + 1) for r, c in inner + edge]


def make_kernel(gx, gy, listed):
    ring_y = gy + 2
    lines = group_lines(gx, gy)
    count = len(lines)

    outer_y = gy + 2 * WIDE

    def kernel(
        place_ref, sums_hbm, mean_hbm, *refs,
    ):
        pieces_hbm, refs = refs[:7], refs[7:]
        members_ref, out_ref, refs = refs[0], refs[1], refs[2:]
        pieces, refs = refs[:7], refs[7:]
        (
            gram_ref, vec_ref, weight_ref, root_ref, inv_ref, upd_ref, norm_ref, vrow_ref,
            sums_ref, mean_ref, targets_ref, factors_ref, target_ref, factor_ref,
            held_ref, stage_ref, piece_sem, side_sem, in_sem, list_sem, out_sem,
        ) = refs
        arrivals = [
            pltpu.make_async_copy(src, dst, piece_sem.at[k])
            for k, (src, dst) in enumerate(zip(pieces_hbm, pieces))
        ]
        for copy in arrivals:
            copy.start()
        sides = [
            pltpu.make_async_copy(sums_hbm, sums_ref, side_sem.at[0]),
            pltpu.make_async_copy(mean_hbm, mean_ref, side_sem.at[1]),
        ]
        for copy in sides:
            copy.start()
        fetch = pltpu.make_async_copy(members_ref, held_ref, in_sem)
        fetch.start()
        own_ref, low_ref, high_ref, left_ref, right_ref, cleft_ref, cright_ref = pieces

        def start_of(row0, col0):
            return lambda r: (r + row0) * outer_y + col0

        def corner_of(col0):
            return lambda r: (r + jnp.where(r >= WIDE, gx, 0)) * outer_y + col0

        out = (gram_ref, vec_ref)
        arrivals[0].wait()
        gram_loop(sliced(own_ref, start_of(WIDE, WIDE), 4), *out)
        for copy in arrivals[1:]:
            copy.wait()
        for n, (i, j) in enumerate(lines):
            r, c = i - 1, j - 1
            if r < 0:
                block = low_ref[WIDE - 1, c, 128:]
            elif r >= gx:
                block = high_ref[0, c, 128:]
            elif c < 0:
                block = left_ref[r, WIDE - 1, 128:]
            elif c >= gy:
                block = right_ref[r, 0, 128:]
            else:
                block = own_ref[r, c, 128:]
            info = block.astype(F32)
            codes = info[2:3].astype(jnp.int32)
            targets_ref[n : n + 1] = (i + codes // 5) * outer_y + j + codes % 5
            factors_ref[n : n + 1] = info[3:4] + info[4:5] + info[5:6]
        copies = [
            pltpu.make_async_copy(targets_ref, target_ref, list_sem.at[0]),
            pltpu.make_async_copy(factors_ref, factor_ref, list_sem.at[1]),
        ]
        for copy in copies:
            copy.start()
        gram_loop(
            [(low_ref, start_of(0, WIDE)), (high_ref, start_of(WIDE + gx, WIDE))], *out
        )
        gram_loop(
            sliced(left_ref, start_of(WIDE, 0), 2)
            + sliced(right_ref, start_of(WIDE, WIDE + gy), 2),
            *out,
        )
        gram_loop(
            sliced(cleft_ref, corner_of(0), 2) + sliced(cright_ref, corner_of(WIDE + gy), 2), *out
        )
        for copy in sides + copies:
            copy.wait()
        sums = jnp.sum(sums_ref[...], axis=0)
        shift = 127.0 / (sums[:, 0:1] / sums[:, 1:2])
        eye = (
            lax.broadcasted_iota(jnp.int32, (128, 128), 0)
            == lax.broadcasted_iota(jnp.int32, (128, 128), 1)
        )

        def update_of(value, g):
            keep(upd_ref, g, jnp.where(eye, 1.5, 0.0) - 0.5 * value)

        def keep(ref, g, value):
            high, low = split(value)
            ref[g, 0] = high
            ref[g, 1] = low

        def pair(ref, g):
            return ref[g, 0], ref[g, 1]

        @pl.loop(0, count // BATCH)
        def _(b):
            for g in range(BATCH):
                line = b * BATCH + g
                total = jnp.zeros((128, 128), F32)
                vsum = jnp.zeros((8, 128), F32)
                for j in range(listed):
                    slot = target_ref[line, j]
                    factor = factor_ref[line, j]
                    total = total + factor * gram_ref[slot]
                    vsum = vsum + factor * vec_ref[slot]
                matrix = total + jnp.where(eye, jnp.broadcast_to(shift, (128, 128)), 0.0)
                norm = jnp.sqrt(jnp.sum(matrix * matrix, keepdims=True))
                norm_ref[g] = jnp.broadcast_to(norm, (8, 128))
                root = matrix / norm
                keep(root_ref, g, root)
                update_of(root, g)
                vrow_ref[g, 0:1] = vsum[0:1] + vsum[1:2]
            for g in range(BATCH):
                upd = pair(upd_ref, g)
                inv_ref[g, 0] = upd[0]
                inv_ref[g, 1] = upd[1]
                keep(root_ref, g, product(pair(root_ref, g), upd))
            for step in range(1, NSI):
                for g in range(BATCH):
                    update_of(product(pair(inv_ref, g), pair(root_ref, g)), g)
                for g in range(BATCH):
                    upd = pair(upd_ref, g)
                    if step < NSI - 1:
                        inv, root = pair(inv_ref, g), pair(root_ref, g)
                        stacked = tuple(
                            jnp.concatenate([i, r], axis=0) for i, r in zip(inv, root)
                        )
                        both = product(stacked, upd)
                        keep(inv_ref, g, both[:128])
                        keep(root_ref, g, both[128:])
                    else:
                        inv = product(pair(inv_ref, g), upd)
                        place = place_ref[b * BATCH + g]
                        norm = norm_ref[g][0:1]
                        once = jnp.sum(inv * vrow_ref[g, 0:1], axis=1, keepdims=True)
                        row = jnp.broadcast_to(once, (128, 128)).T[0:1]
                        wbar = jnp.sum(inv * (row / norm), axis=1, keepdims=True)
                        scale = jnp.sqrt(F32(127.0)) / jnp.sqrt(norm)
                        weight_ref[place] = scale * inv + wbar

        fetch.wait()
        empty = jnp.zeros((128, 128), BF16)

        @pl.loop(0, gx)
        def _(r):
            mean = mean_ref[r].T
            for p in range(gy // 2):
                blends = []
                for c in (2 * p, 2 * p + 1):
                    at = (r + 1) * ring_y + (c + 1)
                    blend = (
                        4.0 * weight_ref[at]
                        + weight_ref[at + ring_y]
                        + weight_ref[at - ring_y]
                        + weight_ref[at + 1]
                        + weight_ref[at - 1]
                    ) * 0.125
                    blends.append(blend.astype(BF16))
                rhs = jnp.concatenate(
                    [
                        jnp.concatenate([blends[0], empty], axis=1),
                        jnp.concatenate([empty, blends[1]], axis=1),
                    ],
                    axis=0,
                )
                lhs = jnp.concatenate([held_ref[r, 2 * p], held_ref[r, 2 * p + 1]], axis=1)
                both = jnp.dot(lhs, rhs, preferred_element_type=F32)
                for side in range(2):
                    c = 2 * p + side
                    value = both[:, 128 * side : 128 * side + 128] + mean[:, c : c + 1]
                    stage_ref[r, c] = value.astype(BF16)
            pltpu.make_async_copy(stage_ref.at[r], out_ref.at[r], out_sem.at[r]).start()

        @pl.loop(0, gx)
        def _(r):
            pltpu.make_async_copy(stage_ref.at[r], out_ref.at[r], out_sem.at[r]).wait()

    return kernel


def analyse(sums, pieces, mean, members, listed):
    gx, gy, _, width = members.shape
    outer = (gx + 2 * WIDE) * (gy + 2 * WIDE)
    lines = group_lines(gx, gy)
    place = jnp.array([i * (gy + 2) + j for i, j in lines], jnp.int32)
    smem = pl.BlockSpec(memory_space=pltpu.SMEM)
    hbm = pl.BlockSpec(memory_space=pltpu.HBM)
    halves = pltpu.VMEM((BATCH, 2, width, width), BF16)
    padded = -(-len(lines) // 8) * 8
    return pl.pallas_call(
        make_kernel(gx, gy, listed),
        name="analyse",
        out_shape=jax.ShapeDtypeStruct(members.shape, BF16),
        in_specs=[smem] + [hbm] * (3 + len(pieces)),
        out_specs=hbm,
        scratch_shapes=[pltpu.VMEM(x.shape, x.dtype) for x in pieces]
        + [
            pltpu.VMEM((outer, width, width), F32),
            pltpu.VMEM((outer, 8, width), F32),
            pltpu.VMEM(((gx + 2) * (gy + 2), width, width), F32),
            halves, halves, halves,
            pltpu.VMEM((BATCH, 8, width), F32),
            pltpu.VMEM((BATCH, 8, width), F32),
            pltpu.VMEM(sums.shape, F32),
            pltpu.VMEM(mean.shape, F32),
            pltpu.VMEM((padded, width), jnp.int32),
            pltpu.VMEM((padded, width), F32),
            pltpu.SMEM((padded, width), jnp.int32),
            pltpu.SMEM((padded, width), F32),
            pltpu.VMEM(members.shape, BF16),
            pltpu.VMEM(members.shape, BF16),
            pltpu.SemaphoreType.DMA((len(pieces),)),
            pltpu.SemaphoreType.DMA((2,)),
            pltpu.SemaphoreType.DMA,
            pltpu.SemaphoreType.DMA((2,)),
            pltpu.SemaphoreType.DMA((gx,)),
        ],
        compiler_params=pltpu.CompilerParams(vmem_limit_bytes=ANALYSE_VMEM),
    )(place, sums, mean, *pieces, members)


def shards(members, mean_state, obs_pert, obs_rinv, innovation, obs_count, neighbours, loc_weight):
    _, gy = obs_pert.shape[:2]
    tx, ty = lax.axis_size(TX), lax.axis_size(TY)
    own, last_x, first_x, last_y, first_y, sums = prepare(
        obs_pert, obs_rinv, innovation, obs_count, neighbours, loc_weight, tx * ty
    )
    low = lax.ppermute(last_x, TX, ring(tx, 1))
    high = lax.ppermute(first_x, TX, ring(tx, -1))
    sums = lax.all_to_all(sums, AXES, 0, 0, tiled=True)
    left = lax.ppermute(last_y, TY, ring(ty, 1))
    right = lax.ppermute(first_y, TY, ring(ty, -1))
    forward = jnp.concatenate([low[:, gy - WIDE :], high[:, gy - WIDE :]], axis=0)
    backward = jnp.concatenate([low[:, :WIDE], high[:, :WIDE]], axis=0)
    corners = (
        lax.ppermute(forward, TY, ring(ty, 1)),
        lax.ppermute(backward, TY, ring(ty, -1)),
    )
    listed = neighbours.shape[-1]
    pieces = (own, low, high, left, right, *corners)
    return analyse(sums, pieces, mean_state, members, listed)


def solution(mesh):
    finer = Mesh(mesh.devices.reshape(4, 4, 8, 2), AXES)
    return jax.shard_map(
        shards,
        mesh=finer,
        in_specs=(
            P(TX, TY, None, None),
            P(TX, TY, None),
            P(TX, TY, None, None),
            P(TX, TY, None),
            P(TX, TY, None),
            P(TX, TY),
            P(TX, TY, None),
            P(TX, TY, None),
        ),
        out_specs=P(TX, TY, None, None),
        check_vma=False,
    )
```

time: 104 us -> 87.8 us (0.84)
  blocking collectives: 0 us -> 23.9 us
  starting transfers between devices: 21.9 us -> 11.7 us
  other arithmetic: 10 us -> 0.12 us
  waiting for transfers between devices: 20.7 us -> 11.8 us
  local copies, waits for them, and re-layouts: 9.95 us -> 1.75 us
  between operations: 1.7 us -> 0.12 us
  Pallas kernels: 39.5 us -> 38.3 us
    all_to_all x0 -> x1, blocking collectives: none -> 23.9 us  [shards(): sums = lax.all_to_all(sums, AXES, 0, 0, tiled=True)]
    all_to_all x1 -> x0, waiting for transfers between devices: 10.5 us -> none  [total_of(): lax.all_to_all(sent, ('x', 'y', 'z'), 0, 0, tiled=True)]
    all_to_all x1 -> x0, starting transfers between devices: 7.57 us -> none  [total_of(): lax.all_to_all(sent, ('x', 'y', 'z'), 0, 0, tiled=True)]
    slice x11 -> x2, local copies, waits for them, and re-layouts: 4.42 us -> 0.14 us  [shards(): backward = jnp.concatenate([low[:, :WIDE], high[:, :WIDE]], axis=0)]
    reduce_sum x3 -> x0, other arithmetic: 3.37 us -> none  [the longest x1 1.84 us: shards(): square_sum = jnp.sum(jnp.square(obs_pert.astype(F32)), axis=-1)]
    ppermute x7 -> x6, starting transfers between devices: 14.4 us -> 11.7 us  [the longest x1 5.82 us: shards(): high = lax.ppermute(first_x, TX, ring(tx, -1))]
    concatenate x2, other arithmetic: 1.8 us -> 0.12 us  [the longest x1 0.06 us: shards(): forward = jnp.concatenate([low[:, gy - WIDE:], high[:, gy - WIDE:]], axis=0)]
    ppermute x7 -> x6, waiting for transfers between devices: 10.1 us -> 11.8 us  [the longest x1 6.68 us: shards(): high = lax.ppermute(first_x, TX, ring(tx, -1))]
  transfers between devices with their start and end apart: 8 -> 6, of which waited for: 3 -> 2; matrix products, arithmetic and copies ran while one was open for 9% -> 0% of each run, Pallas kernels for 0% -> 0%
where the time goes in v1:
time: 87.8 us; the launch traced here: 87.7 us
  Pallas kernels  38.3 us (44%)
  blocking collectives  23.9 us (27%)
  waiting for transfers between devices  11.8 us (13%)
  starting transfers between devices  11.7 us (13%)
  local copies, waits for them, and re-layouts  1.75 us (2%)
    pallas_call x1, Pallas kernels, analyse(): pl.pallas_call(make_kernel(gx, gy, listed), name='analyse', out_shape=jax...  33.7 us
    all_to_all x1, blocking collectives, shards(): sums = lax.all_to_all(sums, AXES, 0, 0, tiled=True)  23.9 us
    ppermute x1, waiting for transfers between devices, shards(): high = lax.ppermute(first_x, TX, ring(tx, -1))  6.68 us
    ppermute x1, starting transfers between devices, shards(): high = lax.ppermute(first_x, TX, ring(tx, -1))  5.82 us
    ppermute x1, waiting for transfers between devices, shards(): low = lax.ppermute(last_x, TX, ring(tx, 1))  5.06 us
    pallas_call x1, Pallas kernels, prepare(): pl.pallas_call(prepare_kernel, name='prepare', out_shape=[blocks(gx, gy),...  4.61 us
    ppermute x1, starting transfers between devices, shards(): lax.ppermute(forward, TY, ring(ty, 1))  3.34 us
    ppermute x1, starting transfers between devices, shards(): left = lax.ppermute(last_y, TY, ring(ty, 1))  2.48 us
  transfers between devices with their start and end apart: 6, of which 2 were waited for; matrix products, arithmetic and copies ran while one was open for 0% of the time, Pallas kernels for 0%

profile of v1, /device:TPU:1, one launch (start us, length us, event | category | flops | bytes accessed | tf_op | source)
XLA Modules:
  0.0 87.7 jit_solution(10653771239276221905)
XLA Ops:
  0.0 4.6 %prepare.1 = (bf16[8,4,144,128]{3,2,1,0:T(8,128)(2,1)}, bf16[3,4,144,128]{3,2,1,0:T(8,128)(2,1)}, bf16[3,4,144,128]{3,2,1,0:T(8,128)(2,1)}, bf16[8,3,144,128]{3,...) custom-call(bf16[8,4,128,128]{3,2,1,0:T(8,128)(2,1)} %pert_hbm.1, ...), custom_call_target="tpu_custom_call" | custom-call | tf_op jit(solution)/shard_map/prepare/pallas_call | solution.py:137
  4.6 0.0 copy-start.6
  4.6 5.8 %collective-permute-start.1 = (bf16[3,4,144,128]{3,2,1,0:T(8,128)(2,1)}, bf16[3,4,144,128]{3,2,1,0:T(8,128)(2,1)S(1)}, u32[]{:S(2)}, u32[]{:S(2)}) collective-permute-start(bf16[3,4,144,128]{3,2,1,0:T(8,128)(2,1)} %get-tuple-element.14), channel_id=1, source_target_pairs={{0,240},{16,0},{32,16},{48,32},{64,48},{80,64},{96,80},{112,96},{1... | collective-permute-start | bytes 1327112 | tf_op jit(solution)/shard_map/ppermute | solution.py:414
  10.5 0.0 collective-permute-start
  10.5 2.5 %collective-permute-start.2 = (bf16[8,3,144,128]{3,2,1,0:T(8,128)(2,1)}, bf16[8,3,144,128]{3,2,1,0:T(8,128)(2,1)S(1)}, u32[]{:S(2)}, u32[]{:S(2)}) collective-permute-start(bf16[8,3,144,128]{3,2,1,0:T(8,128)(2,1)} %get-tuple-element.15), channel_id=1, source_target_pairs={{0,1},{1,2},{2,3},{3,4},{4,5},{5,6},{6,7},{7,8},{8,9},{9,10},{10,1... | collective-permute-start | bytes 2654216 | tf_op jit(solution)/shard_map/ppermute | solution.py:416
  12.9 0.0 collective-permute-start.3
  12.9 6.7 %collective-permute-done.1.refs_2_ = bf16[3,4,144,128]{3,2,1,0:T(8,128)(2,1)S(1)} collective-permute-done((bf16[3,4,144,128]{3,2,1,0:T(8,128)(2,1)}, bf16[3,4,144,128]{3,2,1,0:T(8,128)(2,1)S(1)}, u32[]{:S(2)}, u32[]{:S(2)}) %collective-permute-start.1) | collective-permute-done | bytes 442400 | tf_op jit(solution)/shard_map/ppermute | solution.py:414
  19.6 0.0 copy-start
  19.6 0.1 fusion.1
  19.7 5.1 %collective-permute-done.refs_1_ = bf16[3,4,144,128]{3,2,1,0:T(8,128)(2,1)S(1)} collective-permute-done((bf16[3,4,144,128]{3,2,1,0:T(8,128)(2,1)}, bf16[3,4,144,128]{3,2,1,0:T(8,128)(2,1)S(1)}, u32[]{:S(2)}, u32[]{:S(2)}) %collective-permute-start) | collective-permute-done | bytes 442400 | tf_op jit(solution)/shard_map/ppermute | solution.py:413
  24.8 0.0 copy-start.1
  24.8 0.1 fusion
  24.8 0.1 pad_maximum_fusion
  24.9 3.3 %collective-permute-start.4 = (bf16[6,3,144,128]{3,2,1,0:T(8,128)(2,1)S(1)}, bf16[6,3,144,128]{3,2,1,0:T(8,128)(2,1)S(1)}, u32[]{:S(2)}, u32[]{:S(2)}) collective-permute-start(bf16[6,3,144,128]{3,2,1,0:T(8,128)(2,1)S(1)} %pad_maximum_fusion), channel_id=1, source_target_pairs={{0,1},{1,2},{2,3},{3,4},{4,5},{5,6},{6,7},{7,8},{8,9},{9,10},{10,1... | collective-permute-start | bytes 1990664 | tf_op jit(solution)/shard_map/ppermute | solution.py:421
  28.2 0.1 pad_maximum_fusion.1
  28.3 0.0 collective-permute-start.5
  28.3 0.0 copy-done.6
  28.3 23.9 %all_to_all.5.sums_hbm = f32[256,1,128]{2,1,0:T(1,128)} all-to-all(f32[256,1,128]{2,1,0:T(1,128)S(1)} %copy-done.6), channel_id=1, replica_groups=mesh['x'=4,'y'=4,'z'=8,'c'=2] {'x','y','z','c'}, dimensions={0} | all-to-all | bytes 262144 | tf_op jit(solution)/shard_map/all_to_all | solution.py:415
  52.2 0.0 collective-permute-done.2.refs_3_
  52.2 0.0 copy-start.2
  52.2 0.0 collective-permute-done.3.refs_4_
  52.3 0.0 copy-start.3
  52.3 0.0 collective-permute-done.4.refs_5_
  52.3 0.0 copy-start.4
  52.3 0.0 collective-permute-done.5.refs_6_
  52.3 0.0 copy-start.5
  52.3 0.0 copy-done
  52.3 0.0 copy-done.1
  52.3 0.8 copy-done.2
  53.2 0.3 copy-done.3
  53.5 0.2 copy-done.4
  53.7 0.2 copy-done.5
  53.9 33.7 %analyse.1 = bf16[8,4,512,128]{3,2,1,0:T(8,128)(2,1)} custom-call(s32[56]{0:T(128)} %constant.2.clone.place_ref, f32[256,1,128]{2,1,0:T(1,128)} %all_to_all.5.sums_hbm, f32[8,4,512]{2,1,0:T(4,128)} %mean_hbm.1, bf16[8,4,144,128]{3,2,1,0:T(8,128)(2,1)} %get-tuple-element.12.refs_0_, bf16[3,4,144,128]{3,2,1,0:T(8,128)(2,1)} %copy-done.1, ...), custom_call_target="tpu_custom_call" | custom-call | tf_op jit(solution)/shard_map/analyse/pallas_call | solution.py:375
Async XLA Ops:
  4.6 23.7 %copy-start.6 = (f32[256,1,128]{2,1,0:T(1,128)S(1)}, f32[256,1,128]{2,1,0:T(1,128)}, u32[]{:S(2)}) copy-start(f32[256,1,128]{2,1,0:T(1,128)} %get-tuple-element.11) | copy-start | bytes 393220
  4.6 15.0 %collective-permute-start.1 = (bf16[3,4,144,128]{3,2,1,0:T(8,128)(2,1)}, bf16[3,4,144,128]{3,2,1,0:T(8,128)(2,1)S(1)}, u32[]{:S(2)}, u32[]{:S(2)}) collective-permute-start(bf16[3,4,144,128]{3,2,1,0:T(8,128)(2,1)} %get-tuple-element.14), channel_id=1, source_target_pairs={{0,240},{16,0},{32,16},{48,32},{64,48},{80,64},{96,80},{112,96},{1... | collective-permute-start | bytes 1327112 | tf_op jit(solution)/shard_map/ppermute | solution.py:414
  10.5 14.3 %collective-permute-start = (bf16[3,4,144,128]{3,2,1,0:T(8,128)(2,1)}, bf16[3,4,144,128]{3,2,1,0:T(8,128)(2,1)S(1)}, u32[]{:S(2)}, u32[]{:S(2)}) collective-permute-start(bf16[3,4,144,128]{3,2,1,0:T(8,128)(2,1)} %get-tuple-element.13), channel_id=1, source_target_pairs={{0,16},{16,32},{32,48},{48,64},{64,80},{80,96},{96,112},{112,128},... | collective-permute-start | bytes 1327112 | tf_op jit(solution)/shard_map/ppermute | solution.py:413
  10.5 41.8 %collective-permute-start.2 = (bf16[8,3,144,128]{3,2,1,0:T(8,128)(2,1)}, bf16[8,3,144,128]{3,2,1,0:T(8,128)(2,1)S(1)}, u32[]{:S(2)}, u32[]{:S(2)}) collective-permute-start(bf16[8,3,144,128]{3,2,1,0:T(8,128)(2,1)} %get-tuple-element.15), channel_id=1, source_target_pairs={{0,1},{1,2},{2,3},{3,4},{4,5},{5,6},{6,7},{7,8},{8,9},{9,10},{10,1... | collective-permute-start | bytes 2654216 | tf_op jit(solution)/shard_map/ppermute | solution.py:416
  12.9 39.3 %collective-permute-start.3 = (bf16[8,3,144,128]{3,2,1,0:T(8,128)(2,1)}, bf16[8,3,144,128]{3,2,1,0:T(8,128)(2,1)S(1)}, u32[]{:S(2)}, u32[]{:S(2)}) collective-permute-start(bf16[8,3,144,128]{3,2,1,0:T(8,128)(2,1)} %get-tuple-element.16), channel_id=1, source_target_pairs={{0,15},{1,0},{2,1},{3,2},{4,3},{5,4},{6,5},{7,6},{8,7},{9,8},{10,9... | collective-permute-start | bytes 2654216 | tf_op jit(solution)/shard_map/ppermute | solution.py:417
  19.6 32.7 %copy-start = (bf16[3,4,144,128]{3,2,1,0:T(8,128)(2,1)}, bf16[3,4,144,128]{3,2,1,0:T(8,128)(2,1)S(1)}, u32[]{:S(2)}) copy-start(bf16[3,4,144,128]{3,2,1,0:T(8,128)(2,1)S(1)} %collective-permute-done.1.refs_2_) | copy-start | bytes 1327108
  24.8 27.6 %copy-start.1 = (bf16[3,4,144,128]{3,2,1,0:T(8,128)(2,1)}, bf16[3,4,144,128]{3,2,1,0:T(8,128)(2,1)S(1)}, u32[]{:S(2)}) copy-start(bf16[3,4,144,128]{3,2,1,0:T(8,128)(2,1)S(1)} %collective-permute-done.refs_1_) | copy-start | bytes 1327108
  24.9 27.4 %collective-permute-start.4 = (bf16[6,3,144,128]{3,2,1,0:T(8,128)(2,1)S(1)}, bf16[6,3,144,128]{3,2,1,0:T(8,128)(2,1)S(1)}, u32[]{:S(2)}, u32[]{:S(2)}) collective-permute-start(bf16[6,3,144,128]{3,2,1,0:T(8,128)(2,1)S(1)} %pad_maximum_fusion), channel_id=1, source_target_pairs={{0,1},{1,2},{2,3},{3,4},{4,5},{5,6},{6,7},{7,8},{8,9},{9,10},{10,1... | collective-permute-start | bytes 1990664 | tf_op jit(solution)/shard_map/ppermute | solution.py:421
  28.3 24.0 %collective-permute-start.5 = (bf16[6,3,144,128]{3,2,1,0:T(8,128)(2,1)S(1)}, bf16[6,3,144,128]{3,2,1,0:T(8,128)(2,1)S(1)}, u32[]{:S(2)}, u32[]{:S(2)}) collective-permute-start(bf16[6,3,144,128]{3,2,1,0:T(8,128)(2,1)S(1)} %pad_maximum_fusion.1), channel_id=1, source_target_pairs={{0,15},{1,0},{2,1},{3,2},{4,3},{5,4},{6,5},{7,6},{8,7},{9,8},{10,9... | collective-permute-start | bytes 1990664 | tf_op jit(solution)/shard_map/ppermute | solution.py:422
  52.2 0.9 %copy-start.2 = (bf16[8,3,144,128]{3,2,1,0:T(8,128)(2,1)}, bf16[8,3,144,128]{3,2,1,0:T(8,128)(2,1)S(1)}, u32[]{:S(2)}) copy-start(bf16[8,3,144,128]{3,2,1,0:T(8,128)(2,1)S(1)} %collective-permute-done.2.refs_3_) | copy-start | bytes 2654212
  52.3 1.2 %copy-start.3 = (bf16[8,3,144,128]{3,2,1,0:T(8,128)(2,1)}, bf16[8,3,144,128]{3,2,1,0:T(8,128)(2,1)S(1)}, u32[]{:S(2)}) copy-start(bf16[8,3,144,128]{3,2,1,0:T(8,128)(2,1)S(1)} %collective-permute-done.3.refs_4_) | copy-start | bytes 2654212
  52.3 1.4 %copy-start.4 = (bf16[6,3,144,128]{3,2,1,0:T(8,128)(2,1)}, bf16[6,3,144,128]{3,2,1,0:T(8,128)(2,1)S(1)}, u32[]{:S(2)}) copy-start(bf16[6,3,144,128]{3,2,1,0:T(8,128)(2,1)S(1)} %collective-permute-done.4.refs_5_) | copy-start | bytes 1990660
  52.3 1.6 %copy-start.5 = (bf16[6,3,144,128]{3,2,1,0:T(8,128)(2,1)}, bf16[6,3,144,128]{3,2,1,0:T(8,128)(2,1)S(1)}, u32[]{:S(2)}) copy-start(bf16[6,3,144,128]{3,2,1,0:T(8,128)(2,1)S(1)} %collective-permute-done.5.refs_6_) | copy-start | bytes 1990660

commit v2 on v1

--- a/solution.py
+++ b/solution.py
@@ -122,10 +122,27 @@
     s1 = jnp.sum(first, keepdims=True)
     s2 = jnp.sum(alive, keepdims=True) + jnp.sum(spread, keepdims=True) / 127.0
     sums = jnp.where(lane == 0, s1, jnp.where(lane == 1, s2, 0.0))
-    sums_ref[...] = jnp.broadcast_to(sums.reshape(1, 1, 128), sums_ref.shape)
-
-
-def prepare(obs_pert, obs_rinv, innovation, obs_count, neighbours, loc_weight, devices):
+    sums_ref[...] = sums
+
+
+def combine(own, other, devices):
+    vmem = pl.BlockSpec(memory_space=pltpu.VMEM)
+
+    def kernel(own_ref, other_ref, out_ref):
+        both = own_ref[...] + other_ref[...]
+        out_ref[...] = jnp.broadcast_to(both.reshape(1, 1, 128), out_ref.shape)
+
+    return pl.pallas_call(
+        kernel,
+        name="combine",
+        out_shape=jax.ShapeDtypeStruct((devices, 1, own.shape[1]), F32),
+        in_specs=[vmem, vmem],
+        out_specs=vmem,
+        compiler_params=pltpu.CompilerParams(vmem_limit_bytes=2**20),
+    )(own, other)
+
+
+def prepare(obs_pert, obs_rinv, innovation, obs_count, neighbours, loc_weight):
     gx, gy, _, width = obs_pert.shape
     vmem = pl.BlockSpec(memory_space=pltpu.VMEM)
     hbm = pl.BlockSpec(memory_space=pltpu.HBM)
@@ -139,7 +156,7 @@
         name="prepare",
         out_shape=[
             blocks(gx, gy), blocks(WIDE, gy), blocks(WIDE, gy), blocks(gx, WIDE), blocks(gx, WIDE),
-            jax.ShapeDtypeStruct((devices, 1, width), F32),
+            jax.ShapeDtypeStruct((1, width), F32),
         ],
         in_specs=[hbm, hbm, hbm, smem, hbm, hbm],
         out_specs=[vmem] * 6,
@@ -408,11 +425,14 @@
     _, gy = obs_pert.shape[:2]
     tx, ty = lax.axis_size(TX), lax.axis_size(TY)
     own, last_x, first_x, last_y, first_y, sums = prepare(
-        obs_pert, obs_rinv, innovation, obs_count, neighbours, loc_weight, tx * ty
+        obs_pert, obs_rinv, innovation, obs_count, neighbours, loc_weight
     )
+    cores = lax.axis_size("c")
+    other = lax.ppermute(sums, "c", ring(cores, 1))
     low = lax.ppermute(last_x, TX, ring(tx, 1))
     high = lax.ppermute(first_x, TX, ring(tx, -1))
-    sums = lax.all_to_all(sums, AXES, 0, 0, tiled=True)
+    sums = combine(sums, other, tx * ty // cores)
+    sums = lax.all_to_all(sums, ("x", "y", "z"), 0, 0, tiled=True)
     left = lax.ppermute(last_y, TY, ring(ty, 1))
     right = lax.ppermute(first_y, TY, ring(ty, -1))
     forward = jnp.concatenate([low[:, gy - WIDE :], high[:, gy - WIDE :]], axis=0)

time: 87.8 us -> 87.6 us (level)
  blocking collectives: 23.9 us -> 20.1 us
  starting transfers between devices: 11.7 us -> 14.3 us
    all_to_all x1, blocking collectives: 23.9 us -> 20.1 us  [shards(): sums = lax.all_to_all(sums, ('x', 'y', 'z'), 0, 0, tiled=True)]
    ppermute x0 -> x1, starting transfers between devices: none -> 2.64 us  [shards(): other = lax.ppermute(sums, 'c', ring(cores, 1))]
  transfers between devices with their start and end apart: 6 -> 7, of which waited for: 2 -> 3; matrix products, arithmetic and copies ran while one was open for 0% -> 0% of each run, Pallas kernels for 0% -> 0%
where the time goes in v2:
time: 87.6 us; the launch traced here: 87.4 us
  Pallas kernels  38.2 us (44%)
  blocking collectives  20.1 us (23%)
  starting transfers between devices  14.3 us (16%)
  waiting for transfers between devices  12.6 us (14%)
  local copies, waits for them, and re-layouts  1.74 us (2%)
    pallas_call x1, Pallas kernels, analyse(): pl.pallas_call(make_kernel(gx, gy, listed), name='analyse', out_shape=jax...  33.6 us
    all_to_all x1, blocking collectives, shards(): sums = lax.all_to_all(sums, ('x', 'y', 'z'), 0, 0, tiled=True)  20.1 us
    ppermute x1, waiting for transfers between devices, shards(): high = lax.ppermute(first_x, TX, ring(tx, -1))  6.68 us
    ppermute x1, starting transfers between devices, shards(): high = lax.ppermute(first_x, TX, ring(tx, -1))  5.82 us
    ppermute x1, waiting for transfers between devices, shards(): low = lax.ppermute(last_x, TX, ring(tx, 1))  5.06 us
    pallas_call x1, Pallas kernels, prepare(): pl.pallas_call(prepare_kernel, name='prepare', out_shape=[blocks(gx, gy),...  4.61 us
    ppermute x1, starting transfers between devices, shards(): lax.ppermute(forward, TY, ring(ty, 1))  3.34 us
    ppermute x1, starting transfers between devices, shards(): other = lax.ppermute(sums, 'c', ring(cores, 1))  2.64 us
  transfers between devices with their start and end apart: 7, of which 3 were waited for; matrix products, arithmetic and copies ran while one was open for 0% of the time, Pallas kernels for 0%

profile of v2, /device:TPU:1, one launch (start us, length us, event | category | flops | bytes accessed | tf_op | source)
XLA Modules:
  0.0 87.4 jit_solution(11796237066461772397)
XLA Ops:
  0.0 4.6 %prepare.1 = (bf16[8,4,144,128]{3,2,1,0:T(8,128)(2,1)}, bf16[3,4,144,128]{3,2,1,0:T(8,128)(2,1)}, bf16[3,4,144,128]{3,2,1,0:T(8,128)(2,1)}, bf16[8,3,144,128]{3,...) custom-call(bf16[8,4,128,128]{3,2,1,0:T(8,128)(2,1)} %pert_hbm.1, bf16[8,4,128]{2,1,0:T(4,128)(2,1)} %rinv_hbm.1, ...), custom_call_target="tpu_custom_call" | custom-call | tf_op jit(solution)/shard_map/prepare/pallas_call | solution.py:154
  4.6 0.0 copy-start
  4.6 5.8 %collective-permute-start.2 = (bf16[3,4,144,128]{3,2,1,0:T(8,128)(2,1)}, bf16[3,4,144,128]{3,2,1,0:T(8,128)(2,1)S(1)}, u32[]{:S(2)}, u32[]{:S(2)}) collective-permute-start(bf16[3,4,144,128]{3,2,1,0:T(8,128)(2,1)} %get-tuple-element.14), channel_id=1, source_target_pairs={{0,240},{16,0},{32,16},{48,32},{64,48},{80,64},{96,80},{112,96},{1... | collective-permute-start | bytes 1327112 | tf_op jit(solution)/shard_map/ppermute | solution.py:433
  10.4 0.0 collective-permute-start.1
  10.5 2.5 %collective-permute-start.3 = (bf16[8,3,144,128]{3,2,1,0:T(8,128)(2,1)}, bf16[8,3,144,128]{3,2,1,0:T(8,128)(2,1)S(1)}, u32[]{:S(2)}, u32[]{:S(2)}) collective-permute-start(bf16[8,3,144,128]{3,2,1,0:T(8,128)(2,1)} %get-tuple-element.15), channel_id=1, source_target_pairs={{0,1},{1,2},{2,3},{3,4},{4,5},{5,6},{6,7},{7,8},{8,9},{9,10},{10,1... | collective-permute-start | bytes 2654216 | tf_op jit(solution)/shard_map/ppermute | solution.py:436
  12.9 0.0 collective-permute-start.4
  12.9 6.7 %collective-permute-done.2.refs_2_ = bf16[3,4,144,128]{3,2,1,0:T(8,128)(2,1)S(1)} collective-permute-done((bf16[3,4,144,128]{3,2,1,0:T(8,128)(2,1)}, bf16[3,4,144,128]{3,2,1,0:T(8,128)(2,1)S(1)}, u32[]{:S(2)}, u32[]{:S(2)}) %collective-permute-start.2) | collective-permute-done | bytes 442400 | tf_op jit(solution)/shard_map/ppermute | solution.py:433
  19.6 0.0 copy-start.1
  19.6 0.1 fusion.1
  19.7 5.1 %collective-permute-done.1.refs_1_ = bf16[3,4,144,128]{3,2,1,0:T(8,128)(2,1)S(1)} collective-permute-done((bf16[3,4,144,128]{3,2,1,0:T(8,128)(2,1)}, bf16[3,4,144,128]{3,2,1,0:T(8,128)(2,1)S(1)}, u32[]{:S(2)}, u32[]{:S(2)}) %collective-permute-start.1) | collective-permute-done | bytes 442400 | tf_op jit(solution)/shard_map/ppermute | solution.py:432
  24.8 0.0 copy-start.2
  24.8 0.1 fusion
  24.8 0.1 pad_maximum_fusion
  24.9 3.3 %collective-permute-start.5 = (bf16[6,3,144,128]{3,2,1,0:T(8,128)(2,1)S(1)}, bf16[6,3,144,128]{3,2,1,0:T(8,128)(2,1)S(1)}, u32[]{:S(2)}, u32[]{:S(2)}) collective-permute-start(bf16[6,3,144,128]{3,2,1,0:T(8,128)(2,1)S(1)} %pad_maximum_fusion), channel_id=1, source_target_pairs={{0,1},{1,2},{2,3},{3,4},{4,5},{5,6},{6,7},{7,8},{8,9},{9,10},{10,1... | collective-permute-start | bytes 1990664 | tf_op jit(solution)/shard_map/ppermute | solution.py:441
  28.2 0.1 pad_maximum_fusion.1
  28.3 0.0 collective-permute-start.6
  28.3 0.0 copy-done
  28.3 2.6 %collective-permute-start = (f32[1,128]{1,0:T(1,128)S(1)}, f32[1,128]{1,0:T(1,128)S(1)}, u32[]{:S(2)}, u32[]{:S(2)}) collective-permute-start(f32[1,128]{1,0:T(1,128)S(1)} %copy-done), channel_id=1, source_target_pairs={{0,1},{1,0},{2,3},{3,2},{4,5},{5,4},{6,7},{7,6},{8,9},{9,8},{10,11... | collective-permute-start | bytes 1544 | tf_op jit(solution)/shard_map/ppermute | solution.py:431
  31.0 0.8 collective-permute-done.other_ref
  31.8 20.1 %all_to_all.5.sums_hbm = f32[128,1,128]{2,1,0:T(1,128)} all-to-all(f32[128,1,128]{2,1,0:T(1,128)S(1)} %combine.1), channel_id=1, replica_groups=mesh['x'=4,'y'=4,'z'=8,'c'=2] {'x','y','z'}, dimensions={0} | all-to-all | bytes 131072 | tf_op jit(solution)/shard_map/all_to_all | solution.py:435
  52.0 0.0 collective-permute-done.3.refs_3_
  52.0 0.0 copy-start.3
  52.0 0.0 collective-permute-done.4.refs_4_
  52.0 0.0 copy-start.4
  52.0 0.0 collective-permute-done.5.refs_5_
  52.0 0.0 copy-start.5
  52.0 0.0 collective-permute-done.6.refs_6_
  52.0 0.0 copy-start.6
  52.0 0.0 copy-done.1
  52.0 0.0 copy-done.2
  52.1 0.8 copy-done.3
  52.9 0.3 copy-done.4
  53.2 0.2 copy-done.5
  53.4 0.2 copy-done.6
  53.6 33.6 %analyse.1 = bf16[8,4,512,128]{3,2,1,0:T(8,128)(2,1)} custom-call(s32[56]{0:T(128)} %constant.2.clone.place_ref, f32[128,1,128]{2,1,0:T(1,128)} %all_to_all.5.sums_hbm, f32[8,4,512]{2,1,0:T(4,128)} %mean_hbm.1, bf16[8,4,144,128]{3,2,1,0:T(8,128)(2,1)} %get-tuple-element.12.refs_0_, bf16[3,4,144,128]{3,2,1,0:T(8,128)(2,1)} %copy-done.2, ...), custom_call_target="tpu_custom_call" | custom-call | tf_op jit(solution)/shard_map/analyse/pallas_call | solution.py:392
  (1 shorter events, 0.0 us)
Async XLA Ops:
  4.6 23.7 %copy-start = (f32[1,128]{1,0:T(1,128)S(1)}, f32[1,128]{1,0:T(1,128)}, u32[]{:S(2)}) copy-start(f32[1,128]{1,0:T(1,128)} %get-tuple-element.11.own_ref) | copy-start | bytes 1540
  4.6 15.0 %collective-permute-start.2 = (bf16[3,4,144,128]{3,2,1,0:T(8,128)(2,1)}, bf16[3,4,144,128]{3,2,1,0:T(8,128)(2,1)S(1)}, u32[]{:S(2)}, u32[]{:S(2)}) collective-permute-start(bf16[3,4,144,128]{3,2,1,0:T(8,128)(2,1)} %get-tuple-element.14), channel_id=1, source_target_pairs={{0,240},{16,0},{32,16},{48,32},{64,48},{80,64},{96,80},{112,96},{1... | collective-permute-start | bytes 1327112 | tf_op jit(solution)/shard_map/ppermute | solution.py:433
  10.4 14.3 %collective-permute-start.1 = (bf16[3,4,144,128]{3,2,1,0:T(8,128)(2,1)}, bf16[3,4,144,128]{3,2,1,0:T(8,128)(2,1)S(1)}, u32[]{:S(2)}, u32[]{:S(2)}) collective-permute-start(bf16[3,4,144,128]{3,2,1,0:T(8,128)(2,1)} %get-tuple-element.13), channel_id=1, source_target_pairs={{0,16},{16,32},{32,48},{48,64},{64,80},{80,96},{96,112},{112,128},... | collective-permute-start | bytes 1327112 | tf_op jit(solution)/shard_map/ppermute | solution.py:432
  10.5 41.5 %collective-permute-start.3 = (bf16[8,3,144,128]{3,2,1,0:T(8,128)(2,1)}, bf16[8,3,144,128]{3,2,1,0:T(8,128)(2,1)S(1)}, u32[]{:S(2)}, u32[]{:S(2)}) collective-permute-start(bf16[8,3,144,128]{3,2,1,0:T(8,128)(2,1)} %get-tuple-element.15), channel_id=1, source_target_pairs={{0,1},{1,2},{2,3},{3,4},{4,5},{5,6},{6,7},{7,8},{8,9},{9,10},{10,1... | collective-permute-start | bytes 2654216 | tf_op jit(solution)/shard_map/ppermute | solution.py:436
  12.9 39.0 %collective-permute-start.4 = (bf16[8,3,144,128]{3,2,1,0:T(8,128)(2,1)}, bf16[8,3,144,128]{3,2,1,0:T(8,128)(2,1)S(1)}, u32[]{:S(2)}, u32[]{:S(2)}) collective-permute-start(bf16[8,3,144,128]{3,2,1,0:T(8,128)(2,1)} %get-tuple-element.16), channel_id=1, source_target_pairs={{0,15},{1,0},{2,1},{3,2},{4,3},{5,4},{6,5},{7,6},{8,7},{9,8},{10,9... | collective-permute-start | bytes 2654216 | tf_op jit(solution)/shard_map/ppermute | solution.py:437
  19.6 32.4 %copy-start.1 = (bf16[3,4,144,128]{3,2,1,0:T(8,128)(2,1)}, bf16[3,4,144,128]{3,2,1,0:T(8,128)(2,1)S(1)}, u32[]{:S(2)}) copy-start(bf16[3,4,144,128]{3,2,1,0:T(8,128)(2,1)S(1)} %collective-permute-done.2.refs_2_) | copy-start | bytes 1327108
  24.8 27.3 %copy-start.2 = (bf16[3,4,144,128]{3,2,1,0:T(8,128)(2,1)}, bf16[3,4,144,128]{3,2,1,0:T(8,128)(2,1)S(1)}, u32[]{:S(2)}) copy-start(bf16[3,4,144,128]{3,2,1,0:T(8,128)(2,1)S(1)} %collective-permute-done.1.refs_1_) | copy-start | bytes 1327108
  24.9 27.1 %collective-permute-start.5 = (bf16[6,3,144,128]{3,2,1,0:T(8,128)(2,1)S(1)}, bf16[6,3,144,128]{3,2,1,0:T(8,128)(2,1)S(1)}, u32[]{:S(2)}, u32[]{:S(2)}) collective-permute-start(bf16[6,3,144,128]{3,2,1,0:T(8,128)(2,1)S(1)} %pad_maximum_fusion), channel_id=1, source_target_pairs={{0,1},{1,2},{2,3},{3,4},{4,5},{5,6},{6,7},{7,8},{8,9},{9,10},{10,1... | collective-permute-start | bytes 1990664 | tf_op jit(solution)/shard_map/ppermute | solution.py:441
  28.3 23.7 %collective-permute-start.6 = (bf16[6,3,144,128]{3,2,1,0:T(8,128)(2,1)S(1)}, bf16[6,3,144,128]{3,2,1,0:T(8,128)(2,1)S(1)}, u32[]{:S(2)}, u32[]{:S(2)}) collective-permute-start(bf16[6,3,144,128]{3,2,1,0:T(8,128)(2,1)S(1)} %pad_maximum_fusion.1), channel_id=1, source_target_pairs={{0,15},{1,0},{2,1},{3,2},{4,3},{5,4},{6,5},{7,6},{8,7},{9,8},{10,9... | collective-permute-start | bytes 1990664 | tf_op jit(solution)/shard_map/ppermute | solution.py:442
  28.3 3.5 %collective-permute-start = (f32[1,128]{1,0:T(1,128)S(1)}, f32[1,128]{1,0:T(1,128)S(1)}, u32[]{:S(2)}, u32[]{:S(2)}) collective-permute-start(f32[1,128]{1,0:T(1,128)S(1)} %copy-done), channel_id=1, source_target_pairs={{0,1},{1,0},{2,3},{3,2},{4,5},{5,4},{6,7},{7,6},{8,9},{9,8},{10,11... | collective-permute-start | bytes 1544 | tf_op jit(solution)/shard_map/ppermute | solution.py:431
  52.0 0.9 %copy-start.3 = (bf16[8,3,144,128]{3,2,1,0:T(8,128)(2,1)}, bf16[8,3,144,128]{3,2,1,0:T(8,128)(2,1)S(1)}, u32[]{:S(2)}) copy-start(bf16[8,3,144,128]{3,2,1,0:T(8,128)(2,1)S(1)} %collective-permute-done.3.refs_3_) | copy-start | bytes 2654212
  52.0 1.2 %copy-start.4 = (bf16[8,3,144,128]{3,2,1,0:T(8,128)(2,1)}, bf16[8,3,144,128]{3,2,1,0:T(8,128)(2,1)S(1)}, u32[]{:S(2)}) copy-start(bf16[8,3,144,128]{3,2,1,0:T(8,128)(2,1)S(1)} %collective-permute-done.4.refs_4_) | copy-start | bytes 2654212
  52.0 1.4 %copy-start.5 = (bf16[6,3,144,128]{3,2,1,0:T(8,128)(2,1)}, bf16[6,3,144,128]{3,2,1,0:T(8,128)(2,1)S(1)}, u32[]{:S(2)}) copy-start(bf16[6,3,144,128]{3,2,1,0:T(8,128)(2,1)S(1)} %collective-permute-done.5.refs_5_) | copy-start | bytes 1990660
  52.0 1.6 %copy-start.6 = (bf16[6,3,144,128]{3,2,1,0:T(8,128)(2,1)}, bf16[6,3,144,128]{3,2,1,0:T(8,128)(2,1)S(1)}, u32[]{:S(2)}) copy-start(bf16[6,3,144,128]{3,2,1,0:T(8,128)(2,1)S(1)} %collective-permute-done.6.refs_6_) | copy-start | bytes 1990660

commit v3 on v2

--- a/solution.py
+++ b/solution.py
@@ -211,6 +211,7 @@
         pieces, refs = refs[:7], refs[7:]
         (
             gram_ref, vec_ref, weight_ref, root_ref, inv_ref, upd_ref, norm_ref, vrow_ref,
+            next_ref, next_vrow_ref, done_ref, done_norm_ref, done_vrow_ref,
             sums_ref, mean_ref, targets_ref, factors_ref, target_ref, factor_ref,
             held_ref, stage_ref, piece_sem, side_sem, in_sem, list_sem, out_sem,
         ) = refs
@@ -227,7 +228,6 @@
         for copy in sides:
             copy.start()
         fetch = pltpu.make_async_copy(members_ref, held_ref, in_sem)
-        fetch.start()
         own_ref, low_ref, high_ref, left_ref, right_ref, cleft_ref, cright_ref = pieces
 
         def start_of(row0, col0):
@@ -241,6 +241,7 @@
         gram_loop(sliced(own_ref, start_of(WIDE, WIDE), 4), *out)
         for copy in arrivals[1:]:
             copy.wait()
+        fetch.start()
         for n, (i, j) in enumerate(lines):
             r, c = i - 1, j - 1
             if r < 0:
@@ -294,32 +295,58 @@
         def pair(ref, g):
             return ref[g, 0], ref[g, 1]
 
-        @pl.loop(0, count // BATCH)
+        batches = count // BATCH
+
+        def gather(line, g, seed):
+            vsum = jnp.broadcast_to(seed, (8, 128))
+            for j in range(listed):
+                vsum = vsum + factor_ref[line, j] * vec_ref[target_ref[line, j]]
+            next_vrow_ref[g, 0:1] = vsum[0:1] + vsum[1:2]
+            for half in range(2):
+                rows = pl.ds(64 * half, 64)
+                total = jnp.broadcast_to(seed, (64, 128))
+                for j in range(listed):
+                    total = total + factor_ref[line, j] * gram_ref[target_ref[line, j], rows, :]
+                next_ref[g, rows, :] = total
+
+        def finish(line, g):
+            inv = done_ref[g]
+            norm = done_norm_ref[g][0:1]
+            once = jnp.sum(inv * done_vrow_ref[g, 0:1], axis=1, keepdims=True)
+            row = jnp.broadcast_to(once, (128, 128)).T[0:1]
+            wbar = jnp.sum(inv * (row / norm), axis=1, keepdims=True)
+            scale = jnp.sqrt(F32(127.0)) / jnp.sqrt(norm)
+            weight_ref[place_ref[line]] = scale * inv + wbar
+
+        for g in range(BATCH):
+            gather(g, g, jnp.zeros((1, 128), F32))
+
+        @pl.loop(0, batches)
         def _(b):
+            ahead = jnp.minimum(b + 1, batches - 1) * BATCH
+            behind = jnp.maximum(b - 1, 0) * BATCH
             for g in range(BATCH):
-                line = b * BATCH + g
-                total = jnp.zeros((128, 128), F32)
-                vsum = jnp.zeros((8, 128), F32)
-                for j in range(listed):
-                    slot = target_ref[line, j]
-                    factor = factor_ref[line, j]
-                    total = total + factor * gram_ref[slot]
-                    vsum = vsum + factor * vec_ref[slot]
-                matrix = total + jnp.where(eye, jnp.broadcast_to(shift, (128, 128)), 0.0)
+                matrix = next_ref[g] + jnp.where(eye, jnp.broadcast_to(shift, (128, 128)), 0.0)
                 norm = jnp.sqrt(jnp.sum(matrix * matrix, keepdims=True))
                 norm_ref[g] = jnp.broadcast_to(norm, (8, 128))
+                vrow_ref[g, 0:1] = next_vrow_ref[g, 0:1]
                 root = matrix / norm
                 keep(root_ref, g, root)
                 update_of(root, g)
-                vrow_ref[g, 0:1] = vsum[0:1] + vsum[1:2]
             for g in range(BATCH):
                 upd = pair(upd_ref, g)
                 inv_ref[g, 0] = upd[0]
                 inv_ref[g, 1] = upd[1]
                 keep(root_ref, g, product(pair(root_ref, g), upd))
+                finish(behind + g, g)
             for step in range(1, NSI):
                 for g in range(BATCH):
-                    update_of(product(pair(inv_ref, g), pair(root_ref, g)), g)
+                    value = product(pair(inv_ref, g), pair(root_ref, g))
+                    update_of(value, g)
+                    if g % 4 == 1 and (step - 1) * 4 + g // 4 < BATCH:
+                        seed = jnp.where(value[0:1] > 3.0e38, 1.0e-30, 0.0)
+                        k = (step - 1) * 4 + g // 4
+                        gather(ahead + k, k, seed)
                 for g in range(BATCH):
                     upd = pair(upd_ref, g)
                     if step < NSI - 1:
@@ -331,14 +358,12 @@
                         keep(inv_ref, g, both[:128])
                         keep(root_ref, g, both[128:])
                     else:
-                        inv = product(pair(inv_ref, g), upd)
-                        place = place_ref[b * BATCH + g]
-                        norm = norm_ref[g][0:1]
-                        once = jnp.sum(inv * vrow_ref[g, 0:1], axis=1, keepdims=True)
-                        row = jnp.broadcast_to(once, (128, 128)).T[0:1]
-                        wbar = jnp.sum(inv * (row / norm), axis=1, keepdims=True)
-                        scale = jnp.sqrt(F32(127.0)) / jnp.sqrt(norm)
-                        weight_ref[place] = scale * inv + wbar
+                        done_ref[g] = product(pair(inv_ref, g), upd)
+                        done_norm_ref[g] = norm_ref[g]
+                        done_vrow_ref[g, 0:1] = vrow_ref[g, 0:1]
+
+        for g in range(BATCH):
+            finish((batches - 1) * BATCH + g, g)
 
         fetch.wait()
         empty = jnp.zeros((128, 128), BF16)
@@ -403,6 +428,11 @@
             halves, halves, halves,
             pltpu.VMEM((BATCH, 8, width), F32),
             pltpu.VMEM((BATCH, 8, width), F32),
+            pltpu.VMEM((BATCH, width, width), F32),
+            pltpu.VMEM((BATCH, 8, width), F32),
+            pltpu.VMEM((BATCH, width, width), F32),
+            pltpu.VMEM((BATCH, 8, width), F32),
+            pltpu.VMEM((BATCH, 8, width), F32),
             pltpu.VMEM(sums.shape, F32),
             pltpu.VMEM(mean.shape, F32),
             pltpu.VMEM((padded, width), jnp.int32),

time: 87.6 us -> 87.3 us (level)
  no operation moved by 1% of the time
where the time goes in v3:
time: 87.3 us; the launch traced here: 87.1 us
  Pallas kernels  37.9 us (43%)
  blocking collectives  20.1 us (23%)
  starting transfers between devices  14.3 us (16%)
  waiting for transfers between devices  12.6 us (14%)
  local copies, waits for them, and re-layouts  1.74 us (2%)
    pallas_call x1, Pallas kernels, analyse(): pl.pallas_call(make_kernel(gx, gy, listed), name='analyse', out_shape=jax...  33.3 us
    all_to_all x1, blocking collectives, shards(): sums = lax.all_to_all(sums, ('x', 'y', 'z'), 0, 0, tiled=True)  20.1 us
    ppermute x1, waiting for transfers between devices, shards(): high = lax.ppermute(first_x, TX, ring(tx, -1))  6.68 us
    ppermute x1, starting transfers between devices, shards(): high = lax.ppermute(first_x, TX, ring(tx, -1))  5.82 us
    ppermute x1, waiting for transfers between devices, shards(): low = lax.ppermute(last_x, TX, ring(tx, 1))  5.06 us
    pallas_call x1, Pallas kernels, prepare(): pl.pallas_call(prepare_kernel, name='prepare', out_shape=[blocks(gx, gy),...  4.61 us
    ppermute x1, starting transfers between devices, shards(): lax.ppermute(forward, TY, ring(ty, 1))  3.34 us
    ppermute x1, starting transfers between devices, shards(): other = lax.ppermute(sums, 'c', ring(cores, 1))  2.64 us
  transfers between devices with their start and end apart: 7, of which 3 were waited for; matrix products, arithmetic and copies ran while one was open for 0% of the time, Pallas kernels for 0%

profile of v3, /device:TPU:1, one launch (start us, length us, event | category | flops | bytes accessed | tf_op | source)
XLA Modules:
  0.0 87.1 jit_solution(11908638474895653126)
XLA Ops:
  0.0 4.6 %prepare.1 = (bf16[8,4,144,128]{3,2,1,0:T(8,128)(2,1)}, bf16[3,4,144,128]{3,2,1,0:T(8,128)(2,1)}, bf16[3,4,144,128]{3,2,1,0:T(8,128)(2,1)}, bf16[8,3,144,128]{3,...) custom-call(bf16[8,4,128,128]{3,2,1,0:T(8,128)(2,1)} %pert_hbm.1, bf16[8,4,128]{2,1,0:T(4,128)(2,1)} %rinv_hbm.1, ...), custom_call_target="tpu_custom_call" | custom-call | tf_op jit(solution)/shard_map/prepare/pallas_call | solution.py:154
  4.6 0.0 copy-start
  4.6 5.8 %collective-permute-start.2 = (bf16[3,4,144,128]{3,2,1,0:T(8,128)(2,1)}, bf16[3,4,144,128]{3,2,1,0:T(8,128)(2,1)S(1)}, u32[]{:S(2)}, u32[]{:S(2)}) collective-permute-start(bf16[3,4,144,128]{3,2,1,0:T(8,128)(2,1)} %get-tuple-element.14), channel_id=1, source_target_pairs={{0,240},{16,0},{32,16},{48,32},{64,48},{80,64},{96,80},{112,96},{1... | collective-permute-start | bytes 1327112 | tf_op jit(solution)/shard_map/ppermute | solution.py:463
  10.4 0.0 collective-permute-start.1
  10.5 2.5 %collective-permute-start.3 = (bf16[8,3,144,128]{3,2,1,0:T(8,128)(2,1)}, bf16[8,3,144,128]{3,2,1,0:T(8,128)(2,1)S(1)}, u32[]{:S(2)}, u32[]{:S(2)}) collective-permute-start(bf16[8,3,144,128]{3,2,1,0:T(8,128)(2,1)} %get-tuple-element.15), channel_id=1, source_target_pairs={{0,1},{1,2},{2,3},{3,4},{4,5},{5,6},{6,7},{7,8},{8,9},{9,10},{10,1... | collective-permute-start | bytes 2654216 | tf_op jit(solution)/shard_map/ppermute | solution.py:466
  12.9 0.0 collective-permute-start.4
  12.9 6.7 %collective-permute-done.2.refs_2_ = bf16[3,4,144,128]{3,2,1,0:T(8,128)(2,1)S(1)} collective-permute-done((bf16[3,4,144,128]{3,2,1,0:T(8,128)(2,1)}, bf16[3,4,144,128]{3,2,1,0:T(8,128)(2,1)S(1)}, u32[]{:S(2)}, u32[]{:S(2)}) %collective-permute-start.2) | collective-permute-done | bytes 442400 | tf_op jit(solution)/shard_map/ppermute | solution.py:463
  19.6 0.0 copy-start.1
  19.6 0.1 fusion.1
  19.7 5.1 %collective-permute-done.1.refs_1_ = bf16[3,4,144,128]{3,2,1,0:T(8,128)(2,1)S(1)} collective-permute-done((bf16[3,4,144,128]{3,2,1,0:T(8,128)(2,1)}, bf16[3,4,144,128]{3,2,1,0:T(8,128)(2,1)S(1)}, u32[]{:S(2)}, u32[]{:S(2)}) %collective-permute-start.1) | collective-permute-done | bytes 442400 | tf_op jit(solution)/shard_map/ppermute | solution.py:462
  24.8 0.0 copy-start.2
  24.8 0.1 fusion
  24.8 0.1 pad_maximum_fusion
  24.9 3.3 %collective-permute-start.5 = (bf16[6,3,144,128]{3,2,1,0:T(8,128)(2,1)S(1)}, bf16[6,3,144,128]{3,2,1,0:T(8,128)(2,1)S(1)}, u32[]{:S(2)}, u32[]{:S(2)}) collective-permute-start(bf16[6,3,144,128]{3,2,1,0:T(8,128)(2,1)S(1)} %pad_maximum_fusion), channel_id=1, source_target_pairs={{0,1},{1,2},{2,3},{3,4},{4,5},{5,6},{6,7},{7,8},{8,9},{9,10},{10,1... | collective-permute-start | bytes 1990664 | tf_op jit(solution)/shard_map/ppermute | solution.py:471
  28.2 0.1 pad_maximum_fusion.1
  28.3 0.0 collective-permute-start.6
  28.3 0.0 copy-done
  28.3 2.6 %collective-permute-start = (f32[1,128]{1,0:T(1,128)S(1)}, f32[1,128]{1,0:T(1,128)S(1)}, u32[]{:S(2)}, u32[]{:S(2)}) collective-permute-start(f32[1,128]{1,0:T(1,128)S(1)} %copy-done), channel_id=1, source_target_pairs={{0,1},{1,0},{2,3},{3,2},{4,5},{5,4},{6,7},{7,6},{8,9},{9,8},{10,11... | collective-permute-start | bytes 1544 | tf_op jit(solution)/shard_map/ppermute | solution.py:461
  31.0 0.8 collective-permute-done.other_ref
  31.8 20.1 %all_to_all.5.sums_hbm = f32[128,1,128]{2,1,0:T(1,128)} all-to-all(f32[128,1,128]{2,1,0:T(1,128)S(1)} %combine.1), channel_id=1, replica_groups=mesh['x'=4,'y'=4,'z'=8,'c'=2] {'x','y','z'}, dimensions={0} | all-to-all | bytes 131072 | tf_op jit(solution)/shard_map/all_to_all | solution.py:465
  52.0 0.0 collective-permute-done.3.refs_3_
  52.0 0.0 copy-start.3
  52.0 0.0 collective-permute-done.4.refs_4_
  52.0 0.0 copy-start.4
  52.0 0.0 collective-permute-done.5.refs_5_
  52.0 0.0 copy-start.5
  52.0 0.0 collective-permute-done.6.refs_6_
  52.0 0.0 copy-start.6
  52.0 0.0 copy-done.1
  52.0 0.0 copy-done.2
  52.1 0.8 copy-done.3
  52.9 0.3 copy-done.4
  53.2 0.2 copy-done.5
  53.4 0.2 copy-done.6
  53.6 33.3 %analyse.1 = bf16[8,4,512,128]{3,2,1,0:T(8,128)(2,1)} custom-call(s32[56]{0:T(128)} %constant.2.clone.place_ref, f32[128,1,128]{2,1,0:T(1,128)} %all_to_all.5.sums_hbm, f32[8,4,512]{2,1,0:T(4,128)} %mean_hbm.1, bf16[8,4,144,128]{3,2,1,0:T(8,128)(2,1)} %get-tuple-element.12.refs_0_, bf16[3,4,144,128]{3,2,1,0:T(8,128)(2,1)} %copy-done.2, ...), custom_call_target="tpu_custom_call" | custom-call | tf_op jit(solution)/shard_map/analyse/pallas_call | solution.py:417
  (1 shorter events, 0.0 us)
Async XLA Ops:
  4.6 23.7 %copy-start = (f32[1,128]{1,0:T(1,128)S(1)}, f32[1,128]{1,0:T(1,128)}, u32[]{:S(2)}) copy-start(f32[1,128]{1,0:T(1,128)} %get-tuple-element.11.own_ref) | copy-start | bytes 1540
  4.6 15.0 %collective-permute-start.2 = (bf16[3,4,144,128]{3,2,1,0:T(8,128)(2,1)}, bf16[3,4,144,128]{3,2,1,0:T(8,128)(2,1)S(1)}, u32[]{:S(2)}, u32[]{:S(2)}) collective-permute-start(bf16[3,4,144,128]{3,2,1,0:T(8,128)(2,1)} %get-tuple-element.14), channel_id=1, source_target_pairs={{0,240},{16,0},{32,16},{48,32},{64,48},{80,64},{96,80},{112,96},{1... | collective-permute-start | bytes 1327112 | tf_op jit(solution)/shard_map/ppermute | solution.py:463
  10.4 14.3 %collective-permute-start.1 = (bf16[3,4,144,128]{3,2,1,0:T(8,128)(2,1)}, bf16[3,4,144,128]{3,2,1,0:T(8,128)(2,1)S(1)}, u32[]{:S(2)}, u32[]{:S(2)}) collective-permute-start(bf16[3,4,144,128]{3,2,1,0:T(8,128)(2,1)} %get-tuple-element.13), channel_id=1, source_target_pairs={{0,16},{16,32},{32,48},{48,64},{64,80},{80,96},{96,112},{112,128},... | collective-permute-start | bytes 1327112 | tf_op jit(solution)/shard_map/ppermute | solution.py:462
  10.5 41.5 %collective-permute-start.3 = (bf16[8,3,144,128]{3,2,1,0:T(8,128)(2,1)}, bf16[8,3,144,128]{3,2,1,0:T(8,128)(2,1)S(1)}, u32[]{:S(2)}, u32[]{:S(2)}) collective-permute-start(bf16[8,3,144,128]{3,2,1,0:T(8,128)(2,1)} %get-tuple-element.15), channel_id=1, source_target_pairs={{0,1},{1,2},{2,3},{3,4},{4,5},{5,6},{6,7},{7,8},{8,9},{9,10},{10,1... | collective-permute-start | bytes 2654216 | tf_op jit(solution)/shard_map/ppermute | solution.py:466
  12.9 39.0 %collective-permute-start.4 = (bf16[8,3,144,128]{3,2,1,0:T(8,128)(2,1)}, bf16[8,3,144,128]{3,2,1,0:T(8,128)(2,1)S(1)}, u32[]{:S(2)}, u32[]{:S(2)}) collective-permute-start(bf16[8,3,144,128]{3,2,1,0:T(8,128)(2,1)} %get-tuple-element.16), channel_id=1, source_target_pairs={{0,15},{1,0},{2,1},{3,2},{4,3},{5,4},{6,5},{7,6},{8,7},{9,8},{10,9... | collective-permute-start | bytes 2654216 | tf_op jit(solution)/shard_map/ppermute | solution.py:467
  19.6 32.4 %copy-start.1 = (bf16[3,4,144,128]{3,2,1,0:T(8,128)(2,1)}, bf16[3,4,144,128]{3,2,1,0:T(8,128)(2,1)S(1)}, u32[]{:S(2)}) copy-start(bf16[3,4,144,128]{3,2,1,0:T(8,128)(2,1)S(1)} %collective-permute-done.2.refs_2_) | copy-start | bytes 1327108
  24.8 27.3 %copy-start.2 = (bf16[3,4,144,128]{3,2,1,0:T(8,128)(2,1)}, bf16[3,4,144,128]{3,2,1,0:T(8,128)(2,1)S(1)}, u32[]{:S(2)}) copy-start(bf16[3,4,144,128]{3,2,1,0:T(8,128)(2,1)S(1)} %collective-permute-done.1.refs_1_) | copy-start | bytes 1327108
  24.9 27.1 %collective-permute-start.5 = (bf16[6,3,144,128]{3,2,1,0:T(8,128)(2,1)S(1)}, bf16[6,3,144,128]{3,2,1,0:T(8,128)(2,1)S(1)}, u32[]{:S(2)}, u32[]{:S(2)}) collective-permute-start(bf16[6,3,144,128]{3,2,1,0:T(8,128)(2,1)S(1)} %pad_maximum_fusion), channel_id=1, source_target_pairs={{0,1},{1,2},{2,3},{3,4},{4,5},{5,6},{6,7},{7,8},{8,9},{9,10},{10,1... | collective-permute-start | bytes 1990664 | tf_op jit(solution)/shard_map/ppermute | solution.py:471
  28.3 23.7 %collective-permute-start.6 = (bf16[6,3,144,128]{3,2,1,0:T(8,128)(2,1)S(1)}, bf16[6,3,144,128]{3,2,1,0:T(8,128)(2,1)S(1)}, u32[]{:S(2)}, u32[]{:S(2)}) collective-permute-start(bf16[6,3,144,128]{3,2,1,0:T(8,128)(2,1)S(1)} %pad_maximum_fusion.1), channel_id=1, source_target_pairs={{0,15},{1,0},{2,1},{3,2},{4,3},{5,4},{6,5},{7,6},{8,7},{9,8},{10,9... | collective-permute-start | bytes 1990664 | tf_op jit(solution)/shard_map/ppermute | solution.py:472
  28.3 3.5 %collective-permute-start = (f32[1,128]{1,0:T(1,128)S(1)}, f32[1,128]{1,0:T(1,128)S(1)}, u32[]{:S(2)}, u32[]{:S(2)}) collective-permute-start(f32[1,128]{1,0:T(1,128)S(1)} %copy-done), channel_id=1, source_target_pairs={{0,1},{1,0},{2,3},{3,2},{4,5},{5,4},{6,7},{7,6},{8,9},{9,8},{10,11... | collective-permute-start | bytes 1544 | tf_op jit(solution)/shard_map/ppermute | solution.py:461
  52.0 0.9 %copy-start.3 = (bf16[8,3,144,128]{3,2,1,0:T(8,128)(2,1)}, bf16[8,3,144,128]{3,2,1,0:T(8,128)(2,1)S(1)}, u32[]{:S(2)}) copy-start(bf16[8,3,144,128]{3,2,1,0:T(8,128)(2,1)S(1)} %collective-permute-done.3.refs_3_) | copy-start | bytes 2654212
  52.0 1.2 %copy-start.4 = (bf16[8,3,144,128]{3,2,1,0:T(8,128)(2,1)}, bf16[8,3,144,128]{3,2,1,0:T(8,128)(2,1)S(1)}, u32[]{:S(2)}) copy-start(bf16[8,3,144,128]{3,2,1,0:T(8,128)(2,1)S(1)} %collective-permute-done.4.refs_4_) | copy-start | bytes 2654212
  52.0 1.4 %copy-start.5 = (bf16[6,3,144,128]{3,2,1,0:T(8,128)(2,1)}, bf16[6,3,144,128]{3,2,1,0:T(8,128)(2,1)S(1)}, u32[]{:S(2)}) copy-start(bf16[6,3,144,128]{3,2,1,0:T(8,128)(2,1)S(1)} %collective-permute-done.5.refs_5_) | copy-start | bytes 1990660
  52.0 1.6 %copy-start.6 = (bf16[6,3,144,128]{3,2,1,0:T(8,128)(2,1)}, bf16[6,3,144,128]{3,2,1,0:T(8,128)(2,1)S(1)}, u32[]{:S(2)}) copy-start(bf16[6,3,144,128]{3,2,1,0:T(8,128)(2,1)S(1)} %collective-permute-done.6.refs_6_) | copy-start | bytes 1990660
